TPU v7x, 8 devices: a whole 2x2x1 slice. The times are simulated.
8 devices in a mesh: dp: 1 (over z), my: 2 (over y), mx: 4 (over x, core).
Axes of the slice: x: 2, y: 2, z: 1, core: 2. Of those that a mesh axis runs over, the one named last changes fastest.
Arguments:
- tokens: bfloat16 [64, 256, 4096], P('dp', None, 'my')
- ln_scale: bfloat16 [4096], P('my')
- w_in: bfloat16 [4096, 28672], P('my', 'mx')
- mlp_bias: bfloat16 [16384], P('mx')
- q_scale: bfloat16 [256], replicated
- k_scale: bfloat16 [256], replicated
- w_out: bfloat16 [20480, 4096], P('mx', 'my')
- attn_out_bias: bfloat16 [4096], P('my')
- mlp_out_bias: bfloat16 [4096], P('my')
Outputs:
- output: bfloat16 [64, 256, 4096], P('dp', None, 'my')
All inputs are finite; a program needn't handle non-finite values.
Results may differ from a plain program's by a relative error of at most 0.011843.
Values are sent between devices in bfloat16 or wider.
A program may use at most 1 GiB of HBM per device.

v0:
```python
import jax
import jax.numpy as jnp
from jax import lax
from jax.sharding import PartitionSpec as P


def head_norm(features, gain_vec):
    feat_f32 = features.astype(jnp.float32)
    centered = feat_f32 - jnp.mean(feat_f32, axis=-1, keepdims=True)
    variance = jnp.mean(jnp.square(centered), axis=-1, keepdims=True)
    return (centered * lax.rsqrt(variance + 1e-6) * gain_vec.astype(jnp.float32)).astype(jnp.bfloat16)


def mix_branches(projected, mlp_bias, q_scale, k_scale):
    batch_rows = projected.shape[0]
    seq_len = projected.shape[1]
    head_dim = q_scale.shape[0]
    ff_blk = mlp_bias.shape[0]
    qkv_blk = (projected.shape[2] - ff_blk) // 3
    head_shape = (batch_rows, seq_len, qkv_blk // head_dim, head_dim)
    queries = head_norm(projected[..., :qkv_blk].reshape(head_shape), q_scale)
    keys_n = head_norm(projected[..., qkv_blk:2 * qkv_blk].reshape(head_shape), k_scale)
    values = projected[..., 2 * qkv_blk:3 * qkv_blk].reshape(head_shape)
    logits = jnp.einsum('bqhd,bkhd->bhqk', queries, keys_n, preferred_element_type=jnp.float32) * head_dim ** -0.5
    attn_prob = jax.nn.softmax(logits, axis=-1).astype(jnp.bfloat16)
    mixed = jnp.einsum('bhqk,bkhd->bqhd', attn_prob, values, preferred_element_type=jnp.float32).astype(jnp.bfloat16)
    mlp_act = jax.nn.gelu(projected[..., 3 * qkv_blk:].astype(jnp.float32) + mlp_bias.astype(jnp.float32), approximate=False).astype(jnp.bfloat16)
    return jnp.concatenate([mixed.reshape(batch_rows, seq_len, qkv_blk), mlp_act], axis=-1)


def solution(mesh):
    width_shards = mesh.shape['my']

    def local_layer(tokens, ln_scale, w_in, mlp_bias, q_scale, k_scale, w_out, attn_out_bias, mlp_out_bias):
        width_total = tokens.shape[2] * width_shards
        tok_f32 = tokens.astype(jnp.float32)
        moments = jnp.stack([jnp.sum(tok_f32, axis=-1), jnp.sum(jnp.square(tok_f32), axis=-1)])
        moments = lax.psum(moments, 'my')
        row_mean = moments[0] / width_total
        variance = moments[1] / width_total - jnp.square(row_mean)
        inv_std = lax.rsqrt(variance + 1e-6)
        normed = ((tok_f32 - row_mean[..., None]) * inv_std[..., None] * ln_scale.astype(jnp.float32)).astype(jnp.bfloat16)
        partial_in = jnp.einsum('bsd,dc->bsc', normed, w_in, preferred_element_type=jnp.float32).astype(jnp.bfloat16)
        projected = lax.psum(partial_in, 'my')
        joined = mix_branches(projected, mlp_bias, q_scale, k_scale)
        partial_out = jnp.einsum('bsc,cd->bsd', joined, w_out, preferred_element_type=jnp.float32).astype(jnp.bfloat16)
        summed = lax.psum(partial_out, 'mx')
        result = summed.astype(jnp.float32) + attn_out_bias.astype(jnp.float32) + mlp_out_bias.astype(jnp.float32) + tok_f32
        return result.astype(jnp.bfloat16)

    specs_in = (P('dp', None, 'my'), P('my'), P('my', 'mx'), P('mx'), P(), P(), P('mx', 'my'), P('my'), P('my'))
    return jax.shard_map(local_layer, mesh=mesh, in_specs=specs_in, out_specs=P('dp', None, 'my'), check_vma=False)
```

profile of v0, /device:TPU:0, one launch (start us, length us, event | category | flops | bytes accessed | tf_op | source)
XLA Modules:
  0.0 8510.8 jit_solution(9747690166491369306)
XLA Ops:
  6.5 26.3 convert_reduce_fusion
  32.8 0.7 pad_maximum_fusion
  33.6 18.7 all-reduce.4.cloned.1.call-done
  52.2 0.9 fusion.45
  53.1 0.8 fusion.46
  54.0 538.4 %convolution_convert_fusion = bf16[64,256,7168]{2,1,0:T(8,128)(2,1)} fusion(bf16[64,256,2048]{2,1,0:T(8,128)(2,1)} %param.9, f32[2048]{0:T(1024)S(1)} %convert_element_type.70, f32[64,256]{1,0:T(8,128)S(1)} %fusion.45, f32[64,256]{1,0:T(8,128)S(1)} %fusion.46, bf16[2048,7168]{1,0:T(8,128)(2,1)} %param.11), kind=kOutput, calls=%fused_computation.31 | convolution fusion | flops 481321549824 | bytes 331489280 | tf_op jit(solution)/shard_map/bsd,dc->bsc/dot_general | solution.py:43
  593.0 0.6 convert_element_type.75
  593.6 0.6 convert_element_type.79
  594.2 0.6 convert_element_type.85
  594.8 5044.0 %all-reduce.6.cloned.1.call-done = bf16[64,256,7168]{2,1,0:T(8,128)(2,1)} async-done(((bf16[64,256,7168]{2,1,0:T(8,128)(2,1)}), bf16[64,256,7168]{2,1,0:T(8,128)(2,1)}) %all-reduce.6.cloned.1.call-update) | async-done | bytes 234881040 | tf_op jit(solution)/shard_map/psum | solution.py:44
  5638.8 87.1 %slice_convert_fusion.1 = (f32[64,256,1024]{2,1,0:T(8,128)}, f32[64,256,1024]{2,1,0:T(8,128)}, bf16[64,256,1024]{2,1,0:T(8,128)(2,1)}) fusion(bf16[64,256,7168]{2,1,0:T(8,128)(2,1)} %all-reduce.6.cloned.1.call-done), kind=kLoop, calls=%fused_computation.51 | loop fusion | flops 33554432 | bytes 268435456 | tf_op jit(solution)/shard_map/convert_element_type | solution.py:8
  5726.0 79.4 reshape.67
  5805.4 25.7 reduce_sum.65
  5831.1 7.8 broadcast_multiply_fusion.1
  5838.8 43.7 multiply_reduce_fusion.1
  5882.6 7.7 add_rsqrt_fusion.1
  5890.3 79.4 reshape.68
  5969.7 25.5 reduce_sum.67
  5995.2 7.8 broadcast_multiply_fusion
  6003.0 43.5 multiply_reduce_fusion
  6046.5 4.5 add_rsqrt_fusion
  6051.0 88.8 %multiply_convert_fusion = (bf16[64,256,4,256]{3,2,1,0:T(4,128)(2,1)}, bf16[64,256,4,256]{3,2,1,0:T(4,128)(2,1)}) fusion(f32[64,256,4,256]{3,2,1,0:T(4,128)} %reshape.68, f32[256]{0:T(256)S(1)} %copy-done.6, f32[64,256,4]{2,1,0:T(8,128)S(1)} %add_rsqrt_fusion, f32[64,256,4]{2,1,0:T(8,128)} %broadcast_multiply_fusion, f32[256]{0:T(256)S(1)} %copy-done.5, ...), kind=kLoop, calls=%fused_computation.39 | loop fusion | flops 134217728 | bytes 202377216 | tf_op jit(solution)/shard_map/convert_element_type | solution.py:11
  6139.8 46.6 fusion.34
  6186.4 66.0 fusion.49
  6252.4 44.2 copy.21
  6296.6 46.0 fusion.41
  6342.6 44.3 copy.22
  6387.0 594.9 %fusion.3 = bf16[64,256,4096]{2,1,0:T(8,128)(2,1)} fusion(bf16[64,256,7168]{2,1,0:T(8,128)(2,1)} %all-reduce.6.cloned.1.call-done, f32[4096]{0:T(1024)S(1)} %copy-done), kind=kLoop, calls=%fused_computation.4 | loop fusion | flops 4496293888 | bytes 268451840 | tf_op jit(solution)/shard_map/convert_element_type | solution.py:27
  6981.9 361.9 %fusion.30 = bf16[64,256,2048]{2,1,0:T(8,128)(2,1)} fusion(bf16[64,256,4096]{2,1,0:T(8,128)(2,1)} %fusion.3, bf16[64,256,1024]{2,1,0:T(8,128)(2,1)} %copy.22, bf16[5120,2048]{1,0:T(8,128)(2,1)} %param.15), kind=kOutput, calls=%fused_computation.48 | convolution fusion | flops 343966482432 | bytes 255852544 | tf_op jit(solution)/shard_map/bsc,cd->bsd/dot_general | solution.py:46
  7343.8 0.7 copy-done.3
  7344.5 1093.7 %all-reduce.8.cloned.1.call-done = bf16[64,256,2048]{2,1,0:T(8,128)(2,1)} async-done(((bf16[64,256,2048]{2,1,0:T(8,128)(2,1)}), bf16[64,256,2048]{2,1,0:T(8,128)(2,1)}) %all-reduce.8.cloned.1.call-update) | async-done | bytes 67108880 | tf_op jit(solution)/shard_map/psum | solution.py:47
  8438.2 65.6 fusion.22
  (26 shorter events, 0.8 us)
Async XLA Ops:
  6.5 27.0 copy-start.2
  6.5 45.7 all-reduce.4.cloned.1.call-start
  33.5 5605.4 %all-reduce.6.cloned.1.call-start = ((), (), s32[]{:S(2)}) async-start(), calls=%async_computation.1 | async-start | bytes 469762048 | tf_op jit(solution)/shard_map/psum | solution.py:44
  592.4 0.7 copy-start.7
  592.4 1.2 copy-start.8
  592.4 1.8 copy-start.1
  592.4 7845.8 %all-reduce.8.cloned.1.call-start = ((), (), s32[]{:S(2)}) async-start(), calls=%async_computation.2 | async-start | bytes 134217728 | tf_op jit(solution)/shard_map/psum | solution.py:47
  5995.2 55.8 copy-start.5
  5995.2 55.8 copy-start.6
  6342.6 44.3 copy-start
  7343.8 0.7 copy-start.3
  7343.8 0.7 copy-start.4
Sparse Core Ops, SparseCore 0:
  33.6 18.5 all-reduce.3
  592.5 5046.2 all-reduce.5
  7344.0 1094.2 all-reduce.7
where the time goes:
time: 8530 us; the launch traced here: 8510 us
  waiting for transfers between devices  6160 us (72%)
  other arithmetic  1100 us (13%)
  matrix products  993 us (12%)
  local copies, waits for them, and re-layouts  248 us (3%)
    psum x1, waiting for transfers between devices, local_layer(): projected = lax.psum(partial_in, 'my')  5040 us
    psum x1, waiting for transfers between devices, local_layer(): summed = lax.psum(partial_out, 'mx')  1090 us
    convert_element_type x1, other arithmetic, mix_branches(): jax.nn.gelu(projected[..., 3 * qkv_blk:].astype(jnp.float32) + mlp_bias.a...  595 us
    dot_general x1, matrix products, local_layer(): jnp.einsum('bsd,dc->bsc', normed, w_in, preferred_element_type=jnp.float32)  538 us
    dot_general x1, matrix products, local_layer(): jnp.einsum('bsc,cd->bsd', joined, w_out, preferred_element_type=jnp.float32)  362 us
  transfers between devices with their start and end apart: 3, of which 3 were waited for; matrix products, arithmetic and copies ran while one was open for 0% of the time, Pallas kernels for 0%

commit v1 on v0

v1 whole, which is shorter than its diff:
```python
import functools

import jax
import jax.numpy as jnp
from jax import lax
from jax.experimental import pallas as pl
from jax.experimental.pallas import tpu as pltpu
from jax.sharding import PartitionSpec as P

MESH = pl.DeviceIdType.MESH
F32, BF16 = jnp.float32, jnp.bfloat16

SEQ, DH, WID = 256, 256, 2048
IMGS, GROUPS = 32, 8
M = IMGS // GROUPS * SEQ
HALF = M // 2
ROWS = IMGS * SEQ
TN = 512
QKV = 1024
UNITS = 4096
NJ = 7
NR = 5
NN = WID // TN
T1, T2 = 2 * NJ, 2 * NN
TT = T1 + T2
JB = NR * TN
EPS = 1e-6


def in_col(j, side):
    mlp = (j + 1) // 4
    at = (1 - mlp) * (QKV * j + (QKV // 2) * side) + mlp * (3 * QKV + (UNITS // 2) * side + TN * (j - 3))
    return pl.multiple_of(at, TN)


def out_row(r, side):
    mlp = (r + 3) // 4
    at = (1 - mlp) * (QKV // 2) * side + mlp * (QKV + (UNITS // 2) * side + TN * (r - 1))
    return pl.multiple_of(at, TN)


def tile(n):
    return pl.ds(pl.multiple_of(n * TN, TN), TN)


def rows_of(g):
    return pl.ds(pl.multiple_of(g * M, M), M)


def kernel(tok, lns, w_in, mb, qs, ks, w_out, ob,
           out, toth, wb, wc, wd, w2b, w2c, w2d, py, po, ry, s1, rx,
           z, joined, qk, vv, wbuf, ptile, sv, lbuf, sc, ub, gains,
           wsem, psem, vsem, lsem, csem,
           t_s, t_r, w_s, w_r, w2_s, w2_r, y_s, y_r, x_s, x_r, o_s, o_r, m_s, m_r):
    y = lax.axis_index("my")
    mi = lax.axis_index("mx")
    x, c = mi // 2, mi % 2
    dev_y = {"my": 1 - y, "mx": mi}
    dev_x = {"my": y, "mx": 2 * (1 - x) + c}
    dev_c = {"my": y, "mx": 2 * x + 1 - c}

    barrier = pltpu.get_barrier_semaphore()
    for dev in (dev_y, dev_x, dev_c):
        pl.semaphore_signal(barrier, inc=1, device_id=dev, device_id_type=MESH)
    pl.semaphore_wait(barrier, 3)

    def remote(src, dst, ss, rs, dev):
        return pltpu.make_async_remote_copy(src_ref=src, dst_ref=dst, send_sem=ss, recv_sem=rs, device_id=dev, device_id_type=MESH)

    def half_rows(g):
        return pl.ds(pl.multiple_of(g * M + x * HALF, HALF), HALF)

    def t_dir(g):
        src = tok.at[pl.ds(pl.multiple_of(c * ROWS + g * M + x * HALF, HALF), HALF)]
        return remote(src, toth.at[half_rows(g)], t_s.at[0, g], t_r.at[0, g], dev_y)

    def t_rel(g):
        return remote(toth.at[half_rows(g)], toth.at[half_rows(g)], t_s.at[1, g], t_r.at[1, g], dev_x)

    def w_c(j):
        return remote(w_in.at[:, pl.ds(in_col(j, 1 - y), TN)], wc.at[:, tile(j)], w_s.at[0, j], w_r.at[0, j], dev_y)

    def w_b(j):
        return remote(w_in.at[:, pl.ds(in_col(j, y), TN)], wb.at[:, tile(j)], w_s.at[1, j], w_r.at[1, j], dev_c)

    def w_d(j):
        return remote(wc.at[:, tile(j)], wd.at[:, tile(j)], w_s.at[2, j], w_r.at[2, j], dev_c)

    def w2_c(r):
        return remote(w_out.at[pl.ds(out_row(r, 1 - y), TN)], w2c.at[tile(r)], w2_s.at[0, r], w2_r.at[0, r], dev_y)

    def w2_b(r):
        return remote(w_out.at[pl.ds(out_row(r, y), TN)], w2b.at[tile(r)], w2_s.at[1, r], w2_r.at[1, r], dev_c)

    def w2_d(r):
        return remote(w2c.at[tile(r)], w2d.at[tile(r)], w2_s.at[2, r], w2_r.at[2, r], dev_c)

    def o_y(g, n):
        return remote(po.at[rows_of(g), tile(n)], ry.at[rows_of(g), tile(n)], y_s.at[g, n], y_r.at[g, n], dev_y)

    def o_x(g, n):
        return remote(s1.at[rows_of(g), tile(n)], rx.at[rows_of(g), tile(n)], x_s.at[g, n], x_r.at[g, n], dev_x)

    def out_rows(g):
        return pl.ds(pl.multiple_of(c * ROWS + g * M, M), M)

    def o_c(g, n):
        at = out.at[out_rows(g), tile(n)]
        return remote(at, at, o_s.at[g, n], o_r.at[g, n], dev_c)

    sc_y = remote(lns, sc.at[1], m_s.at[0], m_r.at[0], dev_y)
    my_units = pl.ds(pl.multiple_of(y * (UNITS // 2), UNITS // 2), UNITS // 2)
    ub_c = remote(mb.at[:, my_units], ub.at[1], m_s.at[1], m_r.at[1], dev_c)

    def loop(lo, hi, body):
        def run(i, carry):
            body(i)
            return carry
        lax.fori_loop(lo, hi, run, 0)

    sc_y.start()
    ub_c.start()
    t_dir(0).start()
    loop(0, NJ, lambda j: w_c(j).start())
    t_dir(1).start()
    loop(0, NR, lambda r: w2_c(r).start())
    t_dir(2).start()
    t_dir(3).start()
    loop(0, NJ, lambda j: w_b(j).start())
    loop(0, NR, lambda r: w2_b(r).start())
    small = [
        pltpu.make_async_copy(lns, sc.at[0], csem.at[0]),
        pltpu.make_async_copy(mb.at[:, my_units], ub.at[0], csem.at[1]),
        pltpu.make_async_copy(qs, gains.at[0], csem.at[2]),
        pltpu.make_async_copy(ks, gains.at[1], csem.at[3]),
    ]
    for one in small:
        one.start()
    t_dir(0).wait_recv()
    t_rel(0).start()
    for one in small:
        one.wait()
    sc_y.wait_recv()
    ub_c.wait_recv()

    def w_copies(t_slot, top, bottom, depth):
        return (
            pltpu.make_async_copy(top, wbuf.at[t_slot, pl.ds(0, depth)], wsem.at[t_slot, 0]),
            pltpu.make_async_copy(bottom, wbuf.at[t_slot, pl.ds(depth, depth)], wsem.at[t_slot, 1]),
        )

    def fetch(g, t):
        slot = t % 2
        j, side = t // 2, t % 2

        @pl.when((t < T1) & (side == 0))
        def _():
            @pl.when(g == 0)
            def _():
                w_c(j).wait_recv()
                w_d(j).start()
            for one in w_copies(slot, w_in.at[:, pl.ds(in_col(j, y), TN)], wc.at[:, tile(j)], WID):
                one.start()

        @pl.when((t < T1) & (side == 1))
        def _():
            @pl.when(g == 0)
            def _():
                w_b(j).wait_recv()
                w_d(j).wait_recv()
            for one in w_copies(slot, wb.at[:, tile(j)], wd.at[:, tile(j)], WID):
                one.start()

        @pl.when(t >= T1)
        def _():
            ue = (t - T1 + NN * ((7 - g) // 7)) % T2

            @pl.when(ue < NN)
            def _():
                @pl.when((g == 0) & (ue == 0))
                def _():
                    def relay(r):
                        w2_c(r).wait_recv()
                        w2_d(r).start()
                    loop(0, NR, relay)
                    loop(0, NR, lambda r: w2_d(r).wait_recv())
                for one in w_copies(slot, w2c.at[:, tile(ue)], w2d.at[:, tile(ue)], JB):
                    one.start()

            @pl.when(ue >= NN)
            def _():
                @pl.when((g == 0) & (ue == NN))
                def _():
                    loop(0, NR, lambda r: w2_b(r).wait_recv())
                cols = tile(ue - NN)
                top = w_out.at[pl.ds(out_row(0, y), TN), cols]
                rest = w_out.at[pl.ds(out_row(1, y), JB - TN), cols]
                pltpu.make_async_copy(top, wbuf.at[slot, pl.ds(0, TN)], wsem.at[slot, 2]).start()
                pltpu.make_async_copy(rest, wbuf.at[slot, pl.ds(TN, JB - TN)], wsem.at[slot, 0]).start()
                pltpu.make_async_copy(w2b.at[:, cols], wbuf.at[slot, pl.ds(JB, JB)], wsem.at[slot, 1]).start()

    def arrive1(slot):
        for one in w_copies(slot, wb.at[:, tile(0)], wd.at[:, tile(0)], WID):
            one.wait()

    def arrive2(g, t):
        slot = t % 2
        ue = (t - T1 + NN * ((7 - g) // 7)) % T2

        @pl.when(ue < NN)
        def _():
            for one in w_copies(slot, w2c.at[:, tile(0)], w2d.at[:, tile(0)], JB):
                one.wait()

        @pl.when(ue >= NN)
        def _():
            cols = tile(0)
            pltpu.make_async_copy(w2b.at[pl.ds(0, TN), cols], wbuf.at[slot, pl.ds(0, TN)], wsem.at[slot, 2]).wait()
            pltpu.make_async_copy(w2b.at[pl.ds(0, JB - TN), cols], wbuf.at[slot, pl.ds(TN, JB - TN)], wsem.at[slot, 0]).wait()
            pltpu.make_async_copy(w2b.at[:, cols], wbuf.at[slot, pl.ds(JB, JB)], wsem.at[slot, 1]).wait()

    def fetch_next(g, t):
        nt = t + 1
        ng = g + nt // TT

        @pl.when(ng < GROUPS)
        def _():
            fetch(ng, nt % TT)

    def load(k, src):
        return pltpu.make_async_copy(src, sv.at[k], vsem.at[k])

    def add_loads(g, n):
        return [load(0, py.at[rows_of(g), tile(n)]), load(1, ry.at[rows_of(g), tile(n)])]

    def add_store(g, n):
        return pltpu.make_async_copy(sv.at[3], s1.at[rows_of(g), tile(n)], vsem.at[3])

    def add_load(g, n):
        o_y(g, n).wait_recv()
        for one in add_loads(g, n):
            one.start()

    def add_do(g, n):
        for one in add_loads(g, n):
            one.wait()
        sv[3] = (sv[0].astype(F32) + sv[1].astype(F32)).astype(BF16)
        add_store(g, n).start()

    def add_send(g, n):
        add_store(g, n).wait()
        o_x(g, n).start()

    def fin_loads(g, n):
        return [load(0, s1.at[rows_of(g), tile(n)]), load(1, rx.at[rows_of(g), tile(n)]), load(2, tok.at[out_rows(g), tile(n)])]

    def fin_store(g, n):
        return pltpu.make_async_copy(sv.at[3], out.at[out_rows(g), tile(n)], vsem.at[3])

    def fin_load(g, n):
        o_x(g, n).wait_recv()
        for one in fin_loads(g, n):
            one.start()

    def fin_do(g, n):
        for one in fin_loads(g, n):
            one.wait()
        total = sv[0].astype(F32) + sv[1].astype(F32) + ob[:, tile(n)] + sv[2].astype(F32)
        sv[3] = total.astype(BF16)
        fin_store(g, n).start()

    def fin_send(g, n):
        fin_store(g, n).wait()
        o_c(g, n).start()

    def service(g, t):
        def chain(first, gg, load_, do_, send_):
            u = t - first

            @pl.when((u >= 2) & (u <= 2 * NN) & (u % 2 == 0))
            def _():
                send_(gg, u // 2 - 1)

            @pl.when((u >= 0) & (u < 2 * NN) & (u % 2 == 0))
            def _():
                load_(gg, u // 2)

            @pl.when((u >= 0) & (u < 2 * NN) & (u % 2 == 1))
            def _():
                do_(gg, u // 2)

        @pl.when(g >= 2)
        def _():
            chain(0, g - 2, add_load, add_do, add_send)

        @pl.when(g >= 3)
        def _():
            chain(9, g - 3, fin_load, fin_do, fin_send)

    def l_copies(g, i, slot):
        at = pl.multiple_of(g * M + i * SEQ, SEQ)
        return (
            pltpu.make_async_copy(tok.at[pl.ds(pl.multiple_of(c * ROWS + at, SEQ), SEQ)], lbuf.at[slot, 0], lsem.at[slot, 0]),
            pltpu.make_async_copy(toth.at[pl.ds(at, SEQ)], lbuf.at[slot, 1], lsem.at[slot, 1]),
        )

    def layer_norm(g):
        for one in l_copies(g, 0, 0):
            one.start()

        def image(i):
            slot = i % 2

            @pl.when(i + 1 < M // SEQ)
            def _():
                for one in l_copies(g, i + 1, 1 - slot):
                    one.start()
            for one in l_copies(g, i, slot):
                one.wait()
            step = 64

            def part(k):
                at = pl.ds(pl.multiple_of(k * step, step), step)
                a, b = lbuf[slot, 0, at].astype(F32), lbuf[slot, 1, at].astype(F32)
                mean = (jnp.sum(a, -1, keepdims=True) + jnp.sum(b, -1, keepdims=True)) * (0.5 / WID)
                a, b = a - mean, b - mean
                var = (jnp.sum(a * a, -1, keepdims=True) + jnp.sum(b * b, -1, keepdims=True)) * (0.5 / WID)
                inv = lax.rsqrt(var + EPS)
                to = pl.ds(pl.multiple_of(i * SEQ + k * step, step), step)
                z[to, :WID] = (a * inv * sc[0]).astype(BF16)
                z[to, WID:] = (b * inv * sc[1]).astype(BF16)
            loop(0, SEQ // step, part)
        loop(0, M // SEQ, image)

    def project(slot):
        return (jnp.dot(z[:, :WID], wbuf[slot, :WID], preferred_element_type=F32)
                + jnp.dot(z[:, WID:], wbuf[slot, WID:2 * WID], preferred_element_type=F32)).astype(BF16)

    def around(g, t, compute):
        @pl.when(g > 0)
        def _():
            fetch_next(g, t)
        compute()

        @pl.when(g == 0)
        def _():
            fetch_next(g, t)
        service(g, t)

    def group(g):
        @pl.when((g >= 1) & (g + 3 < GROUPS))
        def _():
            t_dir(g + 3).start()

        t_rel(g).wait_recv()
        layer_norm(g)

        def qk_tile(t):
            def compute():
                arrive1(t % 2)
                h = project(t % 2).astype(F32)
                gain = gains[t // 2]
                for k in range(2):
                    part = h[:, k * DH:(k + 1) * DH]
                    part = part - jnp.mean(part, -1, keepdims=True)
                    var = jnp.mean(part * part, -1, keepdims=True)
                    qk[t // 2, t % 2, :, k * DH:(k + 1) * DH] = (part * lax.rsqrt(var + EPS) * gain).astype(BF16)
            around(g, t, compute)
        loop(0, 4, qk_tile)

        def v_tile(t):
            def compute():
                arrive1(t % 2)
                vv[t % 2] = project(t % 2)
            around(g, t, compute)
        loop(4, 6, v_tile)

        def mlp_tile(t):
            def compute():
                arrive1(t % 2)
                u = t // 2 - 3
                h = project(t % 2).astype(F32) + ub[t % 2, :, tile(u)]
                act = 0.5 * h * (1.0 + lax.erf(h * 0.7071067811865476))
                joined[:, pl.ds(pl.multiple_of((t % 2) * JB + TN + u * TN, TN), TN)] = act.astype(BF16)
            around(g, t, compute)
        loop(6, T1, mlp_tile)

        @pl.when(g == 0)
        def _():
            t_dir(1).wait_recv()
            t_rel(1).start()

        def attend(i):
            at = pl.ds(pl.multiple_of(i * SEQ, SEQ), SEQ)
            for side in range(2):
                for k in range(2):
                    cols = slice(k * DH, (k + 1) * DH)
                    q, kk, v = qk[0, side, at, cols], qk[1, side, at, cols], vv[side, at, cols]
                    lg = lax.dot_general(q, kk, (((1,), (1,)), ((), ())), preferred_element_type=F32) * (DH ** -0.5)
                    e = jnp.exp(lg - jnp.max(lg, -1, keepdims=True))
                    p = (e / jnp.sum(e, -1, keepdims=True)).astype(BF16)
                    mixed = jnp.dot(p, v, preferred_element_type=F32).astype(BF16)
                    joined[at, side * JB + k * DH:side * JB + (k + 1) * DH] = mixed
        loop(0, M // SEQ, attend)

        def p_store(u):
            ue = (u + NN * ((7 - g) // 7)) % T2
            slot = u % 2

            def to(ref, n):
                return pltpu.make_async_copy(ptile.at[slot], ref.at[rows_of(g), tile(n)], psem.at[slot])
            return ue, to

        def p_start(u):
            ue, to = p_store(u)

            @pl.when(ue < NN)
            def _():
                to(po, ue).start()

            @pl.when(ue >= NN)
            def _():
                to(py, ue - NN).start()

        def p_finish(u):
            ue, to = p_store(u)

            @pl.when(ue < NN)
            def _():
                to(po, ue).wait()
                o_y(g, ue).start()

            @pl.when(ue >= NN)
            def _():
                to(py, ue - NN).wait()

        def out_tile(u):
            t = T1 + u

            def compute():
                arrive2(g, t)
                slot = t % 2
                part = (jnp.dot(joined[:, :JB], wbuf[slot, :JB], preferred_element_type=F32)
                        + jnp.dot(joined[:, JB:], wbuf[slot, JB:], preferred_element_type=F32))
                ptile[u % 2] = part.astype(BF16)
                p_start(u)

                @pl.when(u >= 1)
                def _():
                    p_finish(u - 1)
            around(g, t, compute)
        loop(0, T2, out_tile)
        p_finish(T2 - 1)

        @pl.when(g + 2 < GROUPS)
        def _():
            t_dir(g + 2).wait_recv()
            t_rel(g + 2).start()

    fetch(0, 0)
    loop(0, GROUPS, group)

    def whole(gg, load_, do_, send_):
        def one(n):
            load_(gg, n)
            do_(gg, n)
            send_(gg, n)
        loop(0, NN, one)

    whole(GROUPS - 2, add_load, add_do, add_send)
    whole(GROUPS - 3, fin_load, fin_do, fin_send)
    whole(GROUPS - 1, add_load, add_do, add_send)
    whole(GROUPS - 2, fin_load, fin_do, fin_send)
    whole(GROUPS - 1, fin_load, fin_do, fin_send)

    sc_y.wait_send()
    ub_c.wait_send()
    for one in (w_c, w_b, w_d):
        loop(0, NJ, lambda j, one=one: one(j).wait_send())
    for one in (w2_c, w2_b, w2_d):
        loop(0, NR, lambda r, one=one: one(r).wait_send())

    def settle(g):
        t_dir(g).wait_send()
        t_rel(g).wait_send()

        def chunk(n):
            o_y(g, n).wait_send()
            o_x(g, n).wait_send()
            o_c(g, n).wait_send()
            o_c(g, n).wait_recv()
        loop(0, NN, chunk)
    loop(0, GROUPS, settle)


def solution(mesh):
    hbm = pl.BlockSpec(memory_space=pltpu.HBM)
    vmem = pl.BlockSpec(memory_space=pltpu.VMEM)
    dma = pltpu.SemaphoreType.DMA

    def local_layer(tokens, ln_scale, w_in, mlp_bias, q_scale, k_scale, w_out, attn_out_bias, mlp_out_bias):
        images = tokens.shape[0]
        tok = tokens.reshape(images * SEQ, WID)
        row = lambda v: v.astype(F32).reshape(1, -1)
        act = jax.ShapeDtypeStruct((ROWS, WID), BF16)
        in_half = jax.ShapeDtypeStruct((WID, NJ * TN), BF16)
        out_half = jax.ShapeDtypeStruct((JB, WID), BF16)
        shapes = [jax.ShapeDtypeStruct(tok.shape, BF16), act] + [in_half] * 3 + [out_half] * 3 + [act] * 5
        flops = 2 * ROWS * (2 * WID * T1 * TN + 2 * JB * 2 * WID)
        res = pl.pallas_call(
            kernel,
            out_shape=shapes,
            in_specs=[hbm, hbm, hbm, hbm, hbm, hbm, hbm, vmem],
            out_specs=[hbm] * len(shapes),
            scratch_shapes=[
                pltpu.VMEM((M, 2 * WID), BF16),
                pltpu.VMEM((M, 2 * JB), BF16),
                pltpu.VMEM((2, 2, M, TN), BF16),
                pltpu.VMEM((2, M, TN), BF16),
                pltpu.VMEM((2, 2 * JB, TN), BF16),
                pltpu.VMEM((2, M, TN), BF16),
                pltpu.VMEM((4, M, TN), BF16),
                pltpu.VMEM((2, 2, SEQ, WID), BF16),
                pltpu.VMEM((2, 1, WID), F32),
                pltpu.VMEM((2, 1, UNITS // 2), F32),
                pltpu.VMEM((2, 1, DH), F32),
                dma((2, 3)), dma((2,)), dma((4,)), dma((2, 2)), dma((4,)),
                dma((2, GROUPS)), dma((2, GROUPS)), dma((3, NJ)), dma((3, NJ)), dma((3, NR)), dma((3, NR)),
                dma((GROUPS, NN)), dma((GROUPS, NN)), dma((GROUPS, NN)), dma((GROUPS, NN)), dma((GROUPS, NN)), dma((GROUPS, NN)),
                dma((2,)), dma((2,)),
            ],
            compiler_params=pltpu.CompilerParams(collective_id=0, has_side_effects=True, vmem_limit_bytes=63 * 2**20),
            cost_estimate=pl.CostEstimate(flops=flops, bytes_accessed=2**30, transcendentals=0),
            name="layer",
        )(tok, row(ln_scale), w_in, row(mlp_bias), row(q_scale), row(k_scale), w_out, row(attn_out_bias) + row(mlp_out_bias))
        return res[0].reshape(tokens.shape)

    specs_in = (P('dp', None, 'my'), P('my'), P('my', 'mx'), P('mx'), P(), P(), P('mx', 'my'), P('my'), P('my'))
    return jax.shard_map(local_layer, mesh=mesh, in_specs=specs_in, out_specs=P('dp', None, 'my'), check_vma=False)
```

time: 8530 us -> 1840 us (0.22)
  waiting for transfers between devices: 6160 us -> 0 us
  Pallas kernels: 0 us -> 1790 us
  other arithmetic: 1100 us -> 6.36 us
  matrix products: 993 us -> 0 us
  local copies, waits for them, and re-layouts: 248 us -> 44.1 us
    psum x3 -> x0, waiting for transfers between devices: 6160 us -> none  [the longest x1 5040 us: local_layer(): projected = lax.psum(partial_in, 'my')]
    pallas_call x0 -> x1, Pallas kernels: none -> 1790 us  [local_layer(): pl.pallas_call(kernel, out_shape=shapes, in_specs=[hbm, hbm, hbm, hbm, hb...]
    dot_general x4 -> x0, matrix products: 993 us -> none  [the longest x1 538 us: local_layer(): jnp.einsum('bsd,dc->bsc', normed, w_in, preferred_element_type=jnp.float32)]
    convert_element_type x10 -> x0, other arithmetic: 838 us -> none  [the longest x1 595 us: mix_branches(): jax.nn.gelu(projected[..., 3 * qkv_blk:].astype(jnp.float32) + mlp_bias.a...]
    reduce_sum x5 -> x0, other arithmetic: 165 us -> none  [the longest x2 87.2 us: head_norm(): variance = jnp.mean(jnp.square(centered), axis=-1, keepdims=True)]
    convert_element_type x2 -> x0, local copies, waits for them, and re-layouts: 159 us -> none  [head_norm(): feat_f32 = features.astype(jnp.float32)]
    reshape x2 -> x0, local copies, waits for them, and re-layouts: 88.6 us -> none  [the longest x1 44.3 us: mix_branches(): mixed.reshape(batch_rows, seq_len, qkv_blk)]
  transfers between devices with their start and end apart: 3 -> 0, of which waited for: 3 -> 0; matrix products, arithmetic and copies ran while one was open for 0% -> 0% of each run, Pallas kernels for 0% -> 0%
where the time goes in v1:
time: 1840 us
  Pallas kernels  1790 us (97%)
  local copies, waits for them, and re-layouts  44.1 us (2%)
    pallas_call x1, Pallas kernels, local_layer(): pl.pallas_call(kernel, out_shape=shapes, in_specs=[hbm, hbm, hbm, hbm, hb...  1790 us
    unnamed x1, local copies, waits for them, and re-layouts  44.1 us

profile of v1, /device:TPU:0, one launch (start us, length us, event | category | flops | bytes accessed | tf_op | source)
XLA Modules:
  0.0 1835.9 jit_solution(9914255861689288339)
XLA Ops:
  0.0 1.2 reshape.43
  1.2 1.2 reshape.45
  2.5 1.3 reshape.39
  3.8 1.3 convert_add_fusion
  5.1 1.3 reshape.41
  6.4 1785.4 %layer.1 = (bf16[16384,2048]{1,0:T(8,128)(2,1)}, bf16[8192,2048]{1,0:T(8,128)(2,1)}, bf16[2048,3584]{1,0:T(8,128)(2,1)}, bf16[2048,3584]{1,0:T(8,128)(2,1)}, bf1...) custom-call(bf16[16384,2048]{1,0:T(8,128)(2,1)} %bitcast.tok, ...), custom_call_target="tpu_custom_call" | custom-call | flops 824633720832 | bytes 1073741824 | tf_op jit(solution)/shard_map/layer/pallas_call | solution.py:510
  1791.7 44.1 %copy.11 = bf16[64,256,2048]{2,1,0:T(8,128)(2,1)} copy(bf16[64,256,2048]{2,1,0:T(8,128)(2,1)} %bitcast.6) | data formatting | bytes 134217728

commit v2 on v0

v2 whole, which is shorter than its diff:
```python
import jax
import jax.numpy as jnp
from jax import lax
from jax.experimental import pallas as pl
from jax.experimental.pallas import tpu as pltpu
from jax.sharding import PartitionSpec as P

MESH = pl.DeviceIdType.MESH
F32, BF16 = jnp.float32, jnp.bfloat16

SEQ, DH, WID = 256, 256, 2048
M, GROUPS = 1024, 4
ROWS = M * GROUPS
HALF = M // 2
TN = 512
QKV, UNITS = 1024, 4096
NS = 4
NJ = 7
NT = NS * NJ
NN = WID // TN
JB = 5 * TN
KH = 2 * JB
LN = 128
EPS = 1e-6


def in_col(j, side):
    mlp = (j + 1) // 4
    at = (1 - mlp) * (QKV * j + (QKV // 2) * side) + mlp * (3 * QKV + (UNITS // 2) * side + TN * (j - 3))
    return pl.ds(pl.multiple_of(at, TN), TN)


def out_row(part, side):
    if part == 0:
        return pl.ds(pl.multiple_of((QKV // 2) * side, QKV // 2), TN)
    return pl.ds(pl.multiple_of(QKV + (UNITS // 2) * side, QKV), UNITS // 2)


PART_ROWS = (pl.ds(0, TN), pl.ds(TN, JB - TN))


def tile(n):
    return pl.ds(pl.multiple_of(n * TN, TN), TN)


def rows_of(g):
    return pl.ds(pl.multiple_of(g * M, M), M)


def tile_of(t):
    a, b = (t + 24) // 28, t // 24
    j = (1 - a) * (t // 2) + (a - b) * (t // 4 + 1 - 2 * ((t % 4) // 2)) + b * (t // 2 - 7)
    s = (1 - a) * (t % 2) + (a - b) * (t % 4) + b * (2 + t % 2)
    return j, s


def loop(lo, hi, body):
    def run(i, carry):
        body(i)
        return carry
    lax.fori_loop(lo, hi, run, 0)


def start_all(copies):
    for one in copies:
        one.start()


def wait_all(copies):
    for one in copies:
        one.wait()


def kernel(tok, lns, w_in, mb, qs, ks, w_out, ob,
           out, toth, w1t, w1b, w2y, w2n, qkv, jb, pa, pb, ry,
           zj, wbuf, ptile, acc, abuf, sv, lbuf, sc, ub, gains,
           w1sem, w2sem, jsem, psem, asem, vsem, lsem, csem,
           t_s, t_r, w_s, w_r, e_s, e_r, d_s, d_r, y_s, y_r, x_s, x_r, o_s, o_r, m_s, m_r):
    y = lax.axis_index("my")
    mi = lax.axis_index("mx")
    x, c = mi // 2, mi % 2
    dev_y = {"my": 1 - y, "mx": mi}
    dev_x = {"my": y, "mx": 2 * (1 - x) + c}
    dev_c = {"my": y, "mx": 2 * x + 1 - c}
    dev_d = {"my": y, "mx": 2 * (1 - x) + 1 - c}
    row0 = (2 * x + c) * ROWS
    row0_x = (2 * (1 - x) + c) * ROWS

    barrier = pltpu.get_barrier_semaphore()
    for dev in (dev_y, dev_x, dev_c, dev_d):
        pl.semaphore_signal(barrier, inc=1, device_id=dev, device_id_type=MESH)
    pl.semaphore_wait(barrier, 4)

    def remote(src, dst, ss, rs, dev):
        return pltpu.make_async_remote_copy(src_ref=src, dst_ref=dst, send_sem=ss, recv_sem=rs, device_id=dev, device_id_type=MESH)

    def t_dir(k):
        src = tok.at[pl.ds(pl.multiple_of(row0 + k * HALF, HALF), HALF)]
        return remote(src, toth.at[pl.ds(pl.multiple_of(k * HALF, HALF), HALF)], t_s.at[k], t_r.at[k], dev_y)

    def w_c(j):
        return remote(w_in.at[:, in_col(j, 1 - y)], w1b.at[0, :, tile(j)], w_s.at[0, j], w_r.at[0, j], dev_y)

    def w_b(j):
        return remote(w_in.at[:, in_col(j, y)], w1t.at[0, :, tile(j)], w_s.at[1, j], w_r.at[1, j], dev_c)

    def w_d(j):
        return remote(w1b.at[0, :, tile(j)], w1b.at[1, :, tile(j)], w_s.at[2, j], w_r.at[2, j], dev_c)

    def w_e(j):
        return remote(w_in.at[:, in_col(j, y)], w1t.at[1, :, tile(j)], w_s.at[3, j], w_r.at[3, j], dev_x)

    def w_f(j):
        return remote(w1b.at[0, :, tile(j)], w1b.at[2, :, tile(j)], w_s.at[4, j], w_r.at[4, j], dev_x)

    def w_g(j):
        return remote(w1t.at[1, :, tile(j)], w1t.at[2, :, tile(j)], w_s.at[5, j], w_r.at[5, j], dev_c)

    def w_h(j):
        return remote(w1b.at[2, :, tile(j)], w1b.at[3, :, tile(j)], w_s.at[6, j], w_r.at[6, j], dev_c)

    class Two:
        def __init__(self, copies):
            self.copies = copies

        def start(self):
            start_all(self.copies)

        def wait_send(self):
            for one in self.copies:
                one.wait_send()

        def wait_recv(self):
            for one in self.copies:
                one.wait_recv()

    def v_c(n):
        return Two([remote(w_out.at[out_row(p, 1 - y), tile(n)], w2n.at[0, PART_ROWS[p], tile(n)],
                           e_s.at[0, n, p], e_r.at[0, n, p], dev_y) for p in range(2)])

    def v_b(n):
        return Two([remote(w_out.at[out_row(p, y), tile(n)], w2y.at[0, PART_ROWS[p], tile(n)],
                           e_s.at[1, n, p], e_r.at[1, n, p], dev_c) for p in range(2)])

    def v_e(n):
        return Two([remote(w_out.at[out_row(p, y), tile(n)], w2y.at[1, PART_ROWS[p], tile(n)],
                           e_s.at[2, n, p], e_r.at[2, n, p], dev_x) for p in range(2)])

    def v_d(n):
        return remote(w2n.at[0, :, tile(n)], w2n.at[1, :, tile(n)], d_s.at[0, n], d_r.at[0, n], dev_c)

    def v_f(n):
        return remote(w2n.at[0, :, tile(n)], w2n.at[2, :, tile(n)], d_s.at[1, n], d_r.at[1, n], dev_x)

    def v_g(n):
        return remote(w2y.at[1, :, tile(n)], w2y.at[2, :, tile(n)], d_s.at[2, n], d_r.at[2, n], dev_c)

    def v_h(n):
        return remote(w2n.at[2, :, tile(n)], w2n.at[3, :, tile(n)], d_s.at[3, n], d_r.at[3, n], dev_c)

    def o_y(g, n):
        return remote(pb.at[rows_of(g), tile(n)], ry.at[rows_of(g), tile(n)], y_s.at[g, n], y_r.at[g, n], dev_y)

    def part_rows(k):
        return pl.ds(pl.multiple_of(k * HALF, HALF), HALF)

    def own_out(k):
        return pl.ds(pl.multiple_of(row0 + k * HALF, HALF), HALF)

    def o_x(k, n):
        at = out.at[own_out(k), tile(n)]
        return remote(at, at, x_s.at[k, n], x_r.at[k, n], dev_x)

    def o_c(k, n):
        at = out.at[own_out(k), tile(n)]
        return remote(at, at, o_s.at[0, k, n], o_r.at[0, k, n], dev_c)

    def o_f(k, n):
        at = out.at[pl.ds(pl.multiple_of(row0_x + k * HALF, HALF), HALF), tile(n)]
        return remote(at, at, o_s.at[1, k, n], o_r.at[1, k, n], dev_c)

    my_units = pl.ds(pl.multiple_of(y * (UNITS // 2), UNITS // 2), UNITS // 2)
    small_far = [
        remote(lns, sc.at[1], m_s.at[0], m_r.at[0], dev_y),
        remote(mb.at[:, my_units], ub.at[1], m_s.at[1], m_r.at[1], dev_c),
        remote(mb.at[:, my_units], ub.at[2], m_s.at[2], m_r.at[2], dev_x),
        remote(mb.at[:, my_units], ub.at[3], m_s.at[3], m_r.at[3], dev_d),
    ]
    small = [
        pltpu.make_async_copy(lns, sc.at[0], csem.at[0]),
        pltpu.make_async_copy(mb.at[:, my_units], ub.at[0], csem.at[1]),
        pltpu.make_async_copy(qs, gains.at[0], csem.at[2]),
        pltpu.make_async_copy(ks, gains.at[1], csem.at[3]),
    ]

    start_all(small_far)
    loop(0, 4, lambda k: t_dir(k).start())
    loop(0, NJ, lambda j: w_c(j).start())
    loop(4, 8, lambda k: t_dir(k).start())
    loop(0, NN, lambda n: v_c(n).start())
    loop(0, 5, lambda j: w_e(j).start())
    loop(0, NJ, lambda j: w_b(j).start())
    loop(0, NN, lambda n: v_b(n).start())
    start_all(small)
    wait_all(small)
    for one in small_far:
        one.wait_recv()

    def l_copies(g, i, slot):
        at = pl.multiple_of(g * M + i * LN, LN)
        return (
            pltpu.make_async_copy(tok.at[pl.ds(pl.multiple_of(row0 + at, LN), LN)], lbuf.at[slot, 0], lsem.at[slot, 0]),
            pltpu.make_async_copy(toth.at[pl.ds(at, LN)], lbuf.at[slot, 1], lsem.at[slot, 1]),
        )

    def layer_norm(g):
        steps = M // LN
        t_dir(2 * g).wait_recv()
        start_all(l_copies(g, 0, 0))

        def rows(i):
            slot = i % 2

            @pl.when(i == steps // 2 - 1)
            def _():
                t_dir(2 * g + 1).wait_recv()

            @pl.when(i + 1 < steps)
            def _():
                start_all(l_copies(g, i + 1, 1 - slot))
            wait_all(l_copies(g, i, slot))
            step = 64

            def part(k):
                at = pl.ds(pl.multiple_of(k * step, step), step)
                a, b = lbuf[slot, 0, at].astype(F32), lbuf[slot, 1, at].astype(F32)
                mean = (jnp.sum(a, -1, keepdims=True) + jnp.sum(b, -1, keepdims=True)) * (0.5 / WID)
                a, b = a - mean, b - mean
                var = (jnp.sum(a * a, -1, keepdims=True) + jnp.sum(b * b, -1, keepdims=True)) * (0.5 / WID)
                inv = lax.rsqrt(var + EPS)
                to = pl.ds(pl.multiple_of(i * LN + k * step, step), step)
                zj[g % 2, to, :WID] = (a * inv * sc[0]).astype(BF16)
                zj[g % 2, to, WID:2 * WID] = (b * inv * sc[1]).astype(BF16)
            loop(0, LN // step, part)
        loop(0, steps, rows)

    def w1_copies(slot, top, bottom):
        return (
            pltpu.make_async_copy(top, wbuf.at[slot, :WID], w1sem.at[slot, 0]),
            pltpu.make_async_copy(bottom, wbuf.at[slot, WID:2 * WID], w1sem.at[slot, 1]),
        )

    def fetch1(p, t):
        j, s = tile_of(t)
        slot = t % 2

        @pl.when(p == 0)
        def _():
            @pl.when(s == 0)
            def _():
                w_c(j).wait_recv()
                w_d(j).start()
                w_f(j).start()

                @pl.when((j == 1) | (j == 3))
                def _():
                    w_e((j + 9) // 2).start()

                @pl.when(j == NJ - 1)
                def _():
                    v_e(0).start()
                    v_e(1).start()

            @pl.when(s == 1)
            def _():
                w_b(j).wait_recv()
                w_d(j).wait_recv()

            @pl.when(s == 2)
            def _():
                w_e(j).wait_recv()
                w_g(j).start()
                w_f(j).wait_recv()
                w_h(j).start()

            @pl.when(s == 3)
            def _():
                w_g(j).wait_recv()
                w_h(j).wait_recv()

        @pl.when(s == 0)
        def _():
            start_all(w1_copies(slot, w_in.at[:, in_col(j, y)], w1b.at[0, :, tile(j)]))

        @pl.when(s > 0)
        def _():
            start_all(w1_copies(slot, w1t.at[s - 1, :, tile(j)], w1b.at[s, :, tile(j)]))

    def h_store(slot, dst):
        return pltpu.make_async_copy(ptile.at[slot], dst, psem.at[slot])

    def h_done(slot):
        h_store(slot, pb.at[rows_of(0), tile(0)]).wait()

    def w1_tile(p, t):
        j, s = tile_of(t)
        wait_all(w1_copies(t % 2, w1t.at[0, :, tile(0)], w1b.at[0, :, tile(0)]))

        def one(gl):
            g = 2 * p + gl

            def project():
                h = (jnp.dot(zj[gl, :, :WID], wbuf[t % 2, :WID], preferred_element_type=F32)
                     + jnp.dot(zj[gl, :, WID:2 * WID], wbuf[t % 2, WID:2 * WID], preferred_element_type=F32))
                return h.astype(BF16)

            @pl.when((t > 0) & (t != 24))
            def _():
                h_done(gl)

            @pl.when(j < 2)
            def _():
                h = project().astype(F32)
                gain = gains[j]
                for k in range(2):
                    part = h[:, k * DH:(k + 1) * DH]
                    part = part - jnp.mean(part, -1, keepdims=True)
                    var = jnp.mean(part * part, -1, keepdims=True)
                    ptile[gl, :, k * DH:(k + 1) * DH] = (part * lax.rsqrt(var + EPS) * gain).astype(BF16)

            @pl.when(j == 2)
            def _():
                ptile[gl] = project()

            @pl.when(j > 2)
            def _():
                h = project().astype(F32) + ub[s, :, tile(j - 3)]
                ptile[gl] = (0.5 * h * (1.0 + lax.erf(h * 0.7071067811865476))).astype(BF16)

            @pl.when(j <= 2)
            def _():
                h_store(gl, qkv.at[j, s, rows_of(g)]).start()

            @pl.when(j > 2)
            def _():
                h_store(gl, jb.at[rows_of(g), pl.ds(pl.multiple_of(s * JB + (j - 2) * TN, TN), TN)]).start()
        loop(0, 2, one)

    def a_loads(p, w, slot):
        g, s = 2 * p + w // NS, w % NS
        return [pltpu.make_async_copy(qkv.at[i, s, rows_of(g)], abuf.at[slot, i], asem.at[slot, i]) for i in range(3)]

    def a_store(p, w, slot):
        g, s = 2 * p + w // NS, w % NS
        return h_store(slot, jb.at[rows_of(g), pl.ds(pl.multiple_of(s * JB, TN), TN)])

    def attention(p):
        units = 2 * NS
        start_all(a_loads(p, 0, 0))

        def unit(w):
            slot = w % 2

            @pl.when(w + 1 < units)
            def _():
                start_all(a_loads(p, w + 1, 1 - slot))
            wait_all(a_loads(p, w, slot))

            @pl.when(w >= 2)
            def _():
                a_store(p, w - 2, slot).wait()

            def images(i):
                for ii in range(2):
                    at = pl.ds(pl.multiple_of((2 * i + ii) * SEQ, SEQ), SEQ)
                    for k in range(2):
                        cols = slice(k * DH, (k + 1) * DH)
                        q, kk, v = abuf[slot, 0, at, cols], abuf[slot, 1, at, cols], abuf[slot, 2, at, cols]
                        lg = lax.dot_general(q, kk, (((1,), (1,)), ((), ())), preferred_element_type=F32) * (DH ** -0.5)
                        e = jnp.exp(lg - jnp.max(lg, -1, keepdims=True))
                        prob = (e / jnp.sum(e, -1, keepdims=True)).astype(BF16)
                        ptile[slot, at, cols] = jnp.dot(prob, v, preferred_element_type=F32).astype(BF16)
            loop(0, M // SEQ // 2, images)
            a_store(p, w, slot).start()
        loop(0, units, unit)
        a_store(p, units - 2, 0).wait()
        a_store(p, units - 1, 1).wait()

    def w2_slot(m, half):
        return 2 * ((m + 1) % 2) + half

    def w2_dst(m, s):
        return wbuf.at[w2_slot(m, s // 2), pl.ds((s % 2) * JB, JB)]

    def fetch2(m):
        n = m // 2
        e = m % 2

        @pl.when(e == 0)
        def _():
            v_d(n).wait_recv()
            v_h(n).wait_recv()
            for s in range(NS):
                pltpu.make_async_copy(w2n.at[s, :, tile(n)], w2_dst(m, s), w2sem.at[e, s]).start()

        @pl.when(e == 1)
        def _():
            v_b(n).wait_recv()
            v_g(n).wait_recv()
            for p in range(2):
                to = wbuf.at[w2_slot(m, 0), PART_ROWS[p]]
                pltpu.make_async_copy(w_out.at[out_row(p, y), tile(n)], to, w2sem.at[e, 4 * p]).start()
            for s in range(1, NS):
                pltpu.make_async_copy(w2y.at[s - 1, :, tile(n)], w2_dst(m, s), w2sem.at[e, s]).start()

    def arrive2(m):
        e = m % 2

        @pl.when(e == 0)
        def _():
            for s in range(NS):
                pltpu.make_async_copy(w2n.at[s, :, tile(0)], w2_dst(m, s), w2sem.at[e, s]).wait()

        @pl.when(e == 1)
        def _():
            for p in range(2):
                to = wbuf.at[w2_slot(m, 0), PART_ROWS[p]]
                pltpu.make_async_copy(w2n.at[0, PART_ROWS[p], tile(0)], to, w2sem.at[e, 4 * p]).wait()
            for s in range(1, NS):
                pltpu.make_async_copy(w2n.at[s, :, tile(0)], w2_dst(m, s), w2sem.at[e, s]).wait()

    def hand_c(n):
        v_c(n).wait_recv()
        v_d(n).start()
        v_f(n).start()

    def hand_e(n):
        v_e(n).wait_recv()
        v_g(n).start()

    def hand_f(n):
        v_f(n).wait_recv()
        v_h(n).start()

    hands = {7: [lambda: hand_c(0)], 10: [lambda: hand_e(0)], 13: [lambda: hand_c(1), lambda: v_e(2).start()],
             16: [lambda: hand_e(1), lambda: hand_f(0)], 19: [lambda: hand_c(2), lambda: v_e(3).start()],
             22: [lambda: hand_f(1)], 25: [lambda: hand_c(3)]}

    def w1_pass(p):
        layer_norm(2 * p)
        layer_norm(2 * p + 1)

        @pl.when(p == 0)
        def _():
            fetch1(p, 0)

        def step(t):
            @pl.when(t == 24)
            def _():
                h_done(0)
                h_done(1)
                attention(p)

            def fetch_next():
                @pl.when(t + 1 < NT)
                def _():
                    fetch1(p, t + 1)

                @pl.when((t + 1 == NT) & (p == 0))
                def _():
                    fetch1(1, 0)

                @pl.when((t + 1 == NT) & (p == 1))
                def _():
                    fetch2(0)

            @pl.when(p == 1)
            def _():
                fetch_next()
            w1_tile(p, t)

            @pl.when(p == 0)
            def _():
                fetch_next()

            for at, todo in hands.items():
                @pl.when((p == 1) & (t == at))
                def _(todo=todo):
                    for one in todo:
                        one()
        loop(0, NT, step)
        h_done(0)
        h_done(1)
    loop(0, 2, w1_pass)

    def load(e, i, src):
        return pltpu.make_async_copy(src, sv.at[e, i], vsem.at[e, i])

    def fin_loads(k, n, e):
        at = (part_rows(k), tile(n))
        return [load(e, 0, pa.at[at]), load(e, 1, ry.at[at]), load(e, 2, tok.at[own_out(k), tile(n)])]

    def fin_store(k, n, e):
        return pltpu.make_async_copy(sv.at[e, 3], out.at[own_out(k), tile(n)], vsem.at[e, 3])

    def fin_load(k, n, e):
        @pl.when(k % 2 == 0)
        def _():
            o_y(k // 2, n).wait_recv()
        start_all(fin_loads(k, n, e))

    def fin_do(k, n, e):
        wait_all(fin_loads(k, n, e))
        total = sv[e, 0].astype(F32) + sv[e, 1].astype(F32) + ob[:, tile(n)] + sv[e, 2].astype(F32)
        sv[e, 3] = total.astype(BF16)
        fin_store(k, n, e).start()

    def fin_send(k, n, e):
        fin_store(k, n, e).wait()
        o_x(k, n).start()
        o_c(k, n).start()

    def hand_out(k, n):
        o_x(k, n).wait_recv()
        o_f(k, n).start()

    fin_at = (16, 32, 52)
    NK = 2 * GROUPS

    def service(v):
        for n, at in enumerate(fin_at):
            i = v - at

            @pl.when((i >= 2) & (i < NK + 2))
            def _(n=n, i=i):
                fin_send(i - 2, n, v % 2)

            @pl.when((i >= 0) & (i < NK))
            def _(n=n, i=i):
                fin_load(i, n, v % 2)

            @pl.when((i >= 1) & (i < NK + 1))
            def _(n=n, i=i):
                fin_do(i - 1, n, (v + 1) % 2)

        @pl.when((v >= 42) & (v < 42 + NK))
        def _():
            hand_out(v - 42, 0)

    def j_copy(v):
        g, half = (v % 8) // 2, v % 2
        src = jb.at[rows_of(g), pl.ds(pl.multiple_of(half * KH, KH), KH)]
        return pltpu.make_async_copy(src, zj.at[half], jsem.at[half])

    def p_copy(m, g):
        n, slot = m // 2, g % 2
        return n, lambda ref: pltpu.make_async_copy(ptile.at[slot], ref.at[rows_of(g), tile(n)], psem.at[slot])

    def p_start(m, g):
        n, to = p_copy(m, g)

        @pl.when(m % 2 == 0)
        def _():
            to(pb).start()

        @pl.when(m % 2 == 1)
        def _():
            to(pa).start()

    def p_finish(m, g):
        n, to = p_copy(m, g)

        @pl.when(m % 2 == 0)
        def _():
            to(pb).wait()
            o_y(g, n).start()

        @pl.when(m % 2 == 1)
        def _():
            to(pa).wait()

    j_copy(0).start()

    def w2_tile(m):
        for at, todo in enumerate((lambda: hand_e(2), lambda: hand_f(2), lambda: hand_e(3), lambda: hand_f(3))):
            @pl.when(m == at)
            def _(todo=todo):
                todo()

        @pl.when(m + 1 < 2 * NN)
        def _():
            fetch2(m + 1)
        arrive2(m)

        def one(g):
            v = m * 2 * GROUPS + 2 * g
            j_copy(v + 1).start()
            j_copy(v).wait()
            acc[...] = jnp.dot(zj[0], wbuf[w2_slot(m, 0)], preferred_element_type=F32)
            service(v)

            @pl.when(v + 2 < 2 * NN * 2 * GROUPS)
            def _():
                j_copy(v + 2).start()
            j_copy(v + 1).wait()
            ptile[g % 2] = (acc[...] + jnp.dot(zj[1], wbuf[w2_slot(m, 1)], preferred_element_type=F32)).astype(BF16)
            p_start(m, g)

            @pl.when(g > 0)
            def _():
                p_finish(m, g - 1)
            service(v + 1)
        loop(0, GROUPS, one)
        p_finish(m, GROUPS - 1)
    loop(0, 2 * NN, w2_tile)

    def last(k):
        hand_out(k, 1)
        fin_load(k, NN - 1, 0)
        fin_do(k, NN - 1, 0)
        fin_send(k, NN - 1, 0)
    loop(0, NK, last)
    loop(0, NK, lambda k: hand_out(k, 2))
    loop(0, NK, lambda k: hand_out(k, 3))

    for one in small_far:
        one.wait_send()
    loop(0, 8, lambda k: t_dir(k).wait_send())
    for one in (w_c, w_b, w_d, w_e, w_f, w_g, w_h):
        loop(0, NJ, lambda j, one=one: one(j).wait_send())
    for one in (v_c, v_b, v_e, v_d, v_f, v_g, v_h):
        loop(0, NN, lambda n, one=one: one(n).wait_send())

    def settle(n):
        loop(0, GROUPS, lambda g: o_y(g, n).wait_send())

        def chunk(k):
            o_x(k, n).wait_send()
            for one in (o_c, o_f):
                one(k, n).wait_send()
                one(k, n).wait_recv()
        loop(0, NK, chunk)
    loop(0, NN, settle)


def solution(mesh):
    hbm = pl.BlockSpec(memory_space=pltpu.HBM)
    vmem = pl.BlockSpec(memory_space=pltpu.VMEM)

    def dma(*shape):
        return pltpu.SemaphoreType.DMA(shape)

    def local_layer(tokens, ln_scale, w_in, mlp_bias, q_scale, k_scale, w_out, attn_out_bias, mlp_out_bias):
        tok = tokens.reshape(-1, WID)
        row = lambda v: v.astype(F32).reshape(1, -1)
        of = lambda *shape: jax.ShapeDtypeStruct(shape, BF16)
        shapes = [of(*tok.shape), of(ROWS, WID), of(3, WID, NJ * TN), of(4, WID, NJ * TN), of(3, JB, WID), of(4, JB, WID),
                  of(3, NS, ROWS, TN), of(ROWS, NS * JB), of(ROWS, WID), of(ROWS, WID), of(ROWS, WID)]
        flops = 2 * ROWS * (2 * WID * NT * TN + NS * JB * 2 * WID)
        pairs = [(8,), (7, NJ), (3, NN, 2), (4, NN), (GROUPS, NN), (2 * GROUPS, NN), (2, 2 * GROUPS, NN), (4,)]
        res = pl.pallas_call(
            kernel,
            out_shape=shapes,
            in_specs=[hbm, hbm, hbm, hbm, hbm, hbm, hbm, vmem],
            out_specs=[hbm] * len(shapes),
            scratch_shapes=[
                pltpu.VMEM((2, M, KH), BF16),
                pltpu.VMEM((4, KH, TN), BF16),
                pltpu.VMEM((2, M, TN), BF16),
                pltpu.VMEM((M, TN), F32),
                pltpu.VMEM((2, 3, M, TN), BF16),
                pltpu.VMEM((2, 4, HALF, TN), BF16),
                pltpu.VMEM((2, 2, LN, WID), BF16),
                pltpu.VMEM((2, 1, WID), F32),
                pltpu.VMEM((NS, 1, UNITS // 2), F32),
                pltpu.VMEM((2, 1, DH), F32),
                dma(2, 2), dma(2, 5), dma(2), dma(2), dma(2, 3), dma(2, 4), dma(2, 2), dma(4),
            ] + [dma(*shape) for shape in pairs for _ in range(2)],
            compiler_params=pltpu.CompilerParams(collective_id=0, has_side_effects=True, vmem_limit_bytes=63 * 2**20),
            cost_estimate=pl.CostEstimate(flops=flops, bytes_accessed=2**30, transcendentals=0),
            name="layer",
        )(tok, row(ln_scale), w_in, row(mlp_bias), row(q_scale), row(k_scale), w_out, row(attn_out_bias) + row(mlp_out_bias))
        return res[0].reshape(tokens.shape)

    specs_in = (P('dp', None, 'my'), P('my'), P('my', 'mx'), P('mx'), P(), P(), P('mx', 'my'), P('my'), P('my'))
    return jax.shard_map(local_layer, mesh=mesh, in_specs=specs_in, out_specs=P('dp', None, 'my'), check_vma=False)
```

time: 8530 us -> 1550 us (0.18)
  waiting for transfers between devices: 6160 us -> 0 us
  Pallas kernels: 0 us -> 1500 us
  other arithmetic: 1100 us -> 6.33 us
  matrix products: 993 us -> 0 us
  local copies, waits for them, and re-layouts: 248 us -> 44.1 us
    psum x3 -> x0, waiting for transfers between devices: 6160 us -> none  [the longest x1 5040 us: local_layer(): projected = lax.psum(partial_in, 'my')]
    pallas_call x0 -> x1, Pallas kernels: none -> 1500 us  [local_layer(): pl.pallas_call(kernel, out_shape=shapes, in_specs=[hbm, hbm, hbm, hbm, hb...]
    dot_general x4 -> x0, matrix products: 993 us -> none  [the longest x1 538 us: local_layer(): jnp.einsum('bsd,dc->bsc', normed, w_in, preferred_element_type=jnp.float32)]
    convert_element_type x10 -> x0, other arithmetic: 838 us -> none  [the longest x1 595 us: mix_branches(): jax.nn.gelu(projected[..., 3 * qkv_blk:].astype(jnp.float32) + mlp_bias.a...]
    reduce_sum x5 -> x0, other arithmetic: 165 us -> none  [the longest x2 87.2 us: head_norm(): variance = jnp.mean(jnp.square(centered), axis=-1, keepdims=True)]
    convert_element_type x2 -> x0, local copies, waits for them, and re-layouts: 159 us -> none  [head_norm(): feat_f32 = features.astype(jnp.float32)]
    reshape x2 -> x0, local copies, waits for them, and re-layouts: 88.6 us -> none  [the longest x1 44.3 us: mix_branches(): mixed.reshape(batch_rows, seq_len, qkv_blk)]
  transfers between devices with their start and end apart: 3 -> 0, of which waited for: 3 -> 0; matrix products, arithmetic and copies ran while one was open for 0% -> 0% of each run, Pallas kernels for 0% -> 0%
where the time goes in v2:
time: 1550 us
  Pallas kernels  1500 us (97%)
  local copies, waits for them, and re-layouts  44.1 us (3%)
    pallas_call x1, Pallas kernels, local_layer(): pl.pallas_call(kernel, out_shape=shapes, in_specs=[hbm, hbm, hbm, hbm, hb...  1500 us
    unnamed x1, local copies, waits for them, and re-layouts  44.1 us

profile of v2, /device:TPU:0, one launch (start us, length us, event | category | flops | bytes accessed | tf_op | source)
XLA Modules:
  0.0 1552.5 jit_solution(14909786074493188406)
XLA Ops:
  0.0 1.2 reshape.43
  1.2 1.2 reshape.45
  2.4 1.3 reshape.39
  3.7 1.3 convert_add_fusion
  5.0 1.3 reshape.41
  6.3 1502.1 %layer.1 = (bf16[16384,2048]{1,0:T(8,128)(2,1)}, bf16[4096,2048]{1,0:T(8,128)(2,1)}, bf16[3,2048,3584]{2,1,0:T(8,128)(2,1)}, bf16[4,2048,3584]{2,1,0:T(8,128)(2,...) custom-call(bf16[16384,2048]{1,0:T(8,128)(2,1)} %bitcast.tok, ...), custom_call_target="tpu_custom_call" | custom-call | flops 824633720832 | bytes 1073741824 | tf_op jit(solution)/shard_map/layer/pallas_call | solution.py:661
  1508.4 44.1 %copy.11 = bf16[64,256,2048]{2,1,0:T(8,128)(2,1)} copy(bf16[64,256,2048]{2,1,0:T(8,128)(2,1)} %bitcast.6) | data formatting | bytes 134217728

commit v3 on v2

--- a/solution.py
+++ b/solution.py
@@ -22,6 +22,8 @@
 KH = 2 * JB
 LN = 128
 EPS = 1e-6
+NK = 2 * GROUPS
+NL = NK // 2
 
 
 def in_col(j, side):
@@ -71,9 +73,9 @@
         one.wait()
 
 
-def kernel(tok, lns, w_in, mb, qs, ks, w_out, ob,
-           out, toth, w1t, w1b, w2y, w2n, qkv, jb, pa, pb, ry,
-           zj, wbuf, ptile, acc, abuf, sv, lbuf, sc, ub, gains,
+def kernel(tok, w_in, w_out, vec,
+           out, tail, toth, w1t, w1b, w2y, w2n, qkv, jb, pa, pb, ry,
+           zj, wbuf, ptile, acc, abuf, sv, lbuf, sc, ub, gains, ob,
            w1sem, w2sem, jsem, psem, asem, vsem, lsem, csem,
            t_s, t_r, w_s, w_r, e_s, e_r, d_s, d_r, y_s, y_r, x_s, x_r, o_s, o_r, m_s, m_r):
     y = lax.axis_index("my")
@@ -98,30 +100,29 @@
         src = tok.at[pl.ds(pl.multiple_of(row0 + k * HALF, HALF), HALF)]
         return remote(src, toth.at[pl.ds(pl.multiple_of(k * HALF, HALF), HALF)], t_s.at[k], t_r.at[k], dev_y)
 
-    def w_c(j):
-        return remote(w_in.at[:, in_col(j, 1 - y)], w1b.at[0, :, tile(j)], w_s.at[0, j], w_r.at[0, j], dev_y)
-
-    def w_b(j):
-        return remote(w_in.at[:, in_col(j, y)], w1t.at[0, :, tile(j)], w_s.at[1, j], w_r.at[1, j], dev_c)
-
-    def w_d(j):
-        return remote(w1b.at[0, :, tile(j)], w1b.at[1, :, tile(j)], w_s.at[2, j], w_r.at[2, j], dev_c)
-
-    def w_e(j):
-        return remote(w_in.at[:, in_col(j, y)], w1t.at[1, :, tile(j)], w_s.at[3, j], w_r.at[3, j], dev_x)
-
-    def w_f(j):
-        return remote(w1b.at[0, :, tile(j)], w1b.at[2, :, tile(j)], w_s.at[4, j], w_r.at[4, j], dev_x)
-
-    def w_g(j):
-        return remote(w1t.at[1, :, tile(j)], w1t.at[2, :, tile(j)], w_s.at[5, j], w_r.at[5, j], dev_c)
-
-    def w_h(j):
-        return remote(w1b.at[2, :, tile(j)], w1b.at[3, :, tile(j)], w_s.at[6, j], w_r.at[6, j], dev_c)
+    C, B, D, E, F, G, H = range(7)
+
+    def w_own(kind, j, side, dst, dev):
+        return remote(w_in.at[:, in_col(j, side)], dst.at[:, tile(j)], w_s.at[kind, j], w_r.at[kind, j], dev)
+
+    def w_pass(kind, j, src, dst, dev):
+        return remote(src.at[:, tile(j)], dst.at[:, tile(j)], w_s.at[kind, j], w_r.at[kind, j], dev)
+
+    tops = [None] + [w1t.at[i] for i in range(NS - 1)]
+    bots = [w1b.at[i] for i in range(NS)]
+    OWN, CORE, FAR, FAR_CORE = range(NS)
+    w_c = lambda j: w_own(C, j, 1 - y, bots[OWN], dev_y)
+    w_b = lambda j: w_own(B, j, y, tops[CORE], dev_c)
+    w_d = lambda j: w_pass(D, j, bots[OWN], bots[CORE], dev_c)
+    w_e = lambda j: w_own(E, j, y, tops[FAR], dev_x)
+    w_f = lambda j: w_pass(F, j, bots[OWN], bots[FAR], dev_x)
+    w_g = lambda j: w_pass(G, j, tops[FAR], tops[FAR_CORE], dev_c)
+    w_h = lambda j: w_pass(H, j, bots[FAR], bots[FAR_CORE], dev_c)
 
     class Two:
-        def __init__(self, copies):
-            self.copies = copies
+        def __init__(self, kind, n, side, dst, dev):
+            self.copies = [remote(w_out.at[out_row(p, side), tile(n)], dst.at[rows, tile(n)], e_s.at[kind, n, p], e_r.at[kind, n, p], dev)
+                           for p, rows in enumerate(PART_ROWS)]
 
         def start(self):
             start_all(self.copies)
@@ -134,29 +135,18 @@
             for one in self.copies:
                 one.wait_recv()
 
-    def v_c(n):
-        return Two([remote(w_out.at[out_row(p, 1 - y), tile(n)], w2n.at[0, PART_ROWS[p], tile(n)],
-                           e_s.at[0, n, p], e_r.at[0, n, p], dev_y) for p in range(2)])
-
-    def v_b(n):
-        return Two([remote(w_out.at[out_row(p, y), tile(n)], w2y.at[0, PART_ROWS[p], tile(n)],
-                           e_s.at[1, n, p], e_r.at[1, n, p], dev_c) for p in range(2)])
-
-    def v_e(n):
-        return Two([remote(w_out.at[out_row(p, y), tile(n)], w2y.at[1, PART_ROWS[p], tile(n)],
-                           e_s.at[2, n, p], e_r.at[2, n, p], dev_x) for p in range(2)])
-
-    def v_d(n):
-        return remote(w2n.at[0, :, tile(n)], w2n.at[1, :, tile(n)], d_s.at[0, n], d_r.at[0, n], dev_c)
-
-    def v_f(n):
-        return remote(w2n.at[0, :, tile(n)], w2n.at[2, :, tile(n)], d_s.at[1, n], d_r.at[1, n], dev_x)
-
-    def v_g(n):
-        return remote(w2y.at[1, :, tile(n)], w2y.at[2, :, tile(n)], d_s.at[2, n], d_r.at[2, n], dev_c)
-
-    def v_h(n):
-        return remote(w2n.at[2, :, tile(n)], w2n.at[3, :, tile(n)], d_s.at[3, n], d_r.at[3, n], dev_c)
+    def v_pass(kind, n, src, dst, dev):
+        return remote(src.at[:, tile(n)], dst.at[:, tile(n)], d_s.at[kind, n], d_r.at[kind, n], dev)
+
+    mine = [None] + [w2y.at[i] for i in range(NS - 1)]
+    theirs = [w2n.at[i] for i in range(NS)]
+    v_c = lambda n: Two(C, n, 1 - y, theirs[OWN], dev_y)
+    v_b = lambda n: Two(B, n, y, mine[CORE], dev_c)
+    v_e = lambda n: Two(D, n, y, mine[FAR], dev_x)
+    v_d = lambda n: v_pass(C, n, theirs[OWN], theirs[CORE], dev_c)
+    v_f = lambda n: v_pass(B, n, theirs[OWN], theirs[FAR], dev_x)
+    v_g = lambda n: v_pass(D, n, mine[FAR], mine[FAR_CORE], dev_c)
+    v_h = lambda n: v_pass(E, n, theirs[FAR], theirs[FAR_CORE], dev_c)
 
     def o_y(g, n):
         return remote(pb.at[rows_of(g), tile(n)], ry.at[rows_of(g), tile(n)], y_s.at[g, n], y_r.at[g, n], dev_y)
@@ -179,19 +169,14 @@
         at = out.at[pl.ds(pl.multiple_of(row0_x + k * HALF, HALF), HALF), tile(n)]
         return remote(at, at, o_s.at[1, k, n], o_r.at[1, k, n], dev_c)
 
-    my_units = pl.ds(pl.multiple_of(y * (UNITS // 2), UNITS // 2), UNITS // 2)
-    small_far = [
-        remote(lns, sc.at[1], m_s.at[0], m_r.at[0], dev_y),
-        remote(mb.at[:, my_units], ub.at[1], m_s.at[1], m_r.at[1], dev_c),
-        remote(mb.at[:, my_units], ub.at[2], m_s.at[2], m_r.at[2], dev_x),
-        remote(mb.at[:, my_units], ub.at[3], m_s.at[3], m_r.at[3], dev_d),
-    ]
-    small = [
-        pltpu.make_async_copy(lns, sc.at[0], csem.at[0]),
-        pltpu.make_async_copy(mb.at[:, my_units], ub.at[0], csem.at[1]),
-        pltpu.make_async_copy(qs, gains.at[0], csem.at[2]),
-        pltpu.make_async_copy(ks, gains.at[1], csem.at[3]),
-    ]
+    lns = vec.at[:, pl.ds(0, WID)]
+    my_units = vec.at[:, pl.ds(pl.multiple_of(WID + y * (UNITS // 2), UNITS // 2), UNITS // 2)]
+    at = WID + UNITS
+    small_far = [remote(src, dst, m_s.at[i], m_r.at[i], dev) for i, (src, dst, dev) in enumerate((
+        (lns, sc.at[1], dev_y), (my_units, ub.at[CORE], dev_c), (my_units, ub.at[FAR], dev_x), (my_units, ub.at[FAR_CORE], dev_d)))]
+    small = [pltpu.make_async_copy(src, dst, csem.at[i]) for i, (src, dst) in enumerate((
+        (lns, sc.at[0]), (my_units, ub.at[OWN]), (vec.at[:, pl.ds(at, DH)], gains.at[0]),
+        (vec.at[:, pl.ds(at + DH, DH)], gains.at[1]), (vec.at[:, pl.ds(at + 2 * DH, WID)], ob)))]
 
     start_all(small_far)
     loop(0, 4, lambda k: t_dir(k).start())
@@ -442,9 +427,9 @@
         v_f(n).wait_recv()
         v_h(n).start()
 
-    hands = {7: [lambda: hand_c(0)], 10: [lambda: hand_e(0)], 13: [lambda: hand_c(1), lambda: v_e(2).start()],
-             16: [lambda: hand_e(1), lambda: hand_f(0)], 19: [lambda: hand_c(2), lambda: v_e(3).start()],
-             22: [lambda: hand_f(1)], 25: [lambda: hand_c(3)]}
+    hands = {5: [lambda: hand_c(0)], 8: [lambda: hand_e(0)], 11: [lambda: hand_c(1), lambda: v_e(2).start()],
+             14: [lambda: hand_e(1), lambda: hand_f(0)], 17: [lambda: hand_c(2), lambda: v_e(3).start()],
+             20: [lambda: hand_f(1)], 23: [lambda: hand_c(3)]}
 
     def w1_pass(p):
         layer_norm(2 * p)
@@ -503,6 +488,12 @@
     def fin_store(k, n, e):
         return pltpu.make_async_copy(sv.at[e, 3], out.at[own_out(k), tile(n)], vsem.at[e, 3])
 
+    def tail_store(k, e):
+        return pltpu.make_async_copy(sv.at[e, 3], tail.at[part_rows(k - NL)], vsem.at[e, 4])
+
+    def is_tail(k, n):
+        return (n == NN - 1) & (k >= NL)
+
     def fin_load(k, n, e):
         @pl.when(k % 2 == 0)
         def _():
@@ -515,37 +506,48 @@
         sv[e, 3] = total.astype(BF16)
         fin_store(k, n, e).start()
 
+        @pl.when(is_tail(k, n))
+        def _():
+            tail_store(k, e).start()
+
     def fin_send(k, n, e):
         fin_store(k, n, e).wait()
-        o_x(k, n).start()
+
+        @pl.when(is_tail(k, n))
+        def _():
+            tail_store(k, e).wait()
+
+        @pl.when(jnp.logical_not(is_tail(k, n)))
+        def _():
+            o_x(k, n).start()
         o_c(k, n).start()
 
     def hand_out(k, n):
         o_x(k, n).wait_recv()
         o_f(k, n).start()
 
-    fin_at = (16, 32, 52)
-    NK = 2 * GROUPS
+    STEPS = 2 * NN * NK
 
     def service(v):
-        for n, at in enumerate(fin_at):
-            i = v - at
-
-            @pl.when((i >= 2) & (i < NK + 2))
-            def _(n=n, i=i):
-                fin_send(i - 2, n, v % 2)
-
-            @pl.when((i >= 0) & (i < NK))
-            def _(n=n, i=i):
-                fin_load(i, n, v % 2)
-
-            @pl.when((i >= 1) & (i < NK + 1))
-            def _(n=n, i=i):
-                fin_do(i - 1, n, (v + 1) % 2)
-
-        @pl.when((v >= 42) & (v < 42 + NK))
-        def _():
-            hand_out(v - 42, 0)
+        f = v - 12
+        n, i = f // 16, f % 16
+
+        @pl.when((f >= 0) & (i >= 2) & (i < NK + 2))
+        def _():
+            fin_send(i - 2, n, v % 2)
+
+        @pl.when((f >= 0) & (i < NK))
+        def _():
+            fin_load(i, n, v % 2)
+
+        @pl.when((f >= 0) & (i >= 1) & (i < NK + 1))
+        def _():
+            fin_do(i - 1, n, (v + 1) % 2)
+
+        for n, at in enumerate((33, 49)):
+            @pl.when((v >= at) & (v < at + NK))
+            def _(n=n, at=at):
+                hand_out(v - at, n)
 
     def j_copy(v):
         g, half = (v % 8) // 2, v % 2
@@ -599,7 +601,7 @@
             acc[...] = jnp.dot(zj[0], wbuf[w2_slot(m, 0)], preferred_element_type=F32)
             service(v)
 
-            @pl.when(v + 2 < 2 * NN * 2 * GROUPS)
+            @pl.when(v + 2 < STEPS)
             def _():
                 j_copy(v + 2).start()
             j_copy(v + 1).wait()
@@ -614,14 +616,9 @@
         p_finish(m, GROUPS - 1)
     loop(0, 2 * NN, w2_tile)
 
-    def last(k):
-        hand_out(k, 1)
-        fin_load(k, NN - 1, 0)
-        fin_do(k, NN - 1, 0)
-        fin_send(k, NN - 1, 0)
-    loop(0, NK, last)
+    loop(STEPS, STEPS + 6, service)
     loop(0, NK, lambda k: hand_out(k, 2))
-    loop(0, NK, lambda k: hand_out(k, 3))
+    loop(0, NK - NL, lambda k: hand_out(k, 3))
 
     for one in small_far:
         one.wait_send()
@@ -635,33 +632,79 @@
         loop(0, GROUPS, lambda g: o_y(g, n).wait_send())
 
         def chunk(k):
+            o_c(k, n).wait_send()
+            o_c(k, n).wait_recv()
+        loop(0, NK, chunk)
+
+        def far_chunk(k):
             o_x(k, n).wait_send()
-            for one in (o_c, o_f):
-                one(k, n).wait_send()
-                one(k, n).wait_recv()
-        loop(0, NK, chunk)
+            o_f(k, n).wait_send()
+            o_f(k, n).wait_recv()
+        loop(0, NK - NL * (n // (NN - 1)), far_chunk)
     loop(0, NN, settle)
+
+
+def copy_kernel(src, dst, buf, sem):
+    slots = buf.shape[0]
+    x = lax.axis_index("mx") // 2
+
+    def moves(i):
+        first = (x + i // (2 * NK)) % 2
+        rows = pl.ds(pl.multiple_of(first * 2 * ROWS + (i % (2 * NK)) * HALF, HALF), HALF)
+        late = i >= 2 * NK and i % NK >= NL
+        cols = pl.ds(0, WID - TN if late else WID)
+        k = i % slots
+        return (pltpu.make_async_copy(src.at[rows, cols], buf.at[k, :, cols], sem.at[0, k]),
+                pltpu.make_async_copy(buf.at[k, :, cols], dst.at[rows, cols], sem.at[1, k]))
+    every = [moves(i) for i in range(4 * NK)]
+    ahead = slots // 2
+    for i in range(4 * NK + ahead):
+        if i < 4 * NK:
+            if i >= slots:
+                every[i - slots][1].wait()
+            every[i][0].start()
+        if i >= ahead:
+            every[i - ahead][0].wait()
+            every[i - ahead][1].start()
+    for i in range(4 * NK - slots, 4 * NK):
+        every[i][1].wait()
+
+
+def tail_kernel(base, far, farther, out, buf, sem):
+    mi = lax.axis_index("mx")
+    x, c = mi // 2, mi % 2
+    pieces = ((far, c), (farther, 1 - c))
+    loads = [pltpu.make_async_copy(ref, buf.at[i], sem.at[0, i]) for i, (ref, _) in enumerate(pieces)]
+    start_all(loads)
+    stores = []
+    for i, (_, cc) in enumerate(pieces):
+        at = pl.multiple_of((2 * (1 - x) + cc) * ROWS + NL * HALF, HALF)
+        store = pltpu.make_async_copy(buf.at[i], out.at[pl.ds(at, (NK - NL) * HALF), pl.ds((NN - 1) * TN, TN)], sem.at[1, i])
+        loads[i].wait()
+        store.start()
+        stores.append(store)
+    wait_all(stores)
 
 
 def solution(mesh):
     hbm = pl.BlockSpec(memory_space=pltpu.HBM)
-    vmem = pl.BlockSpec(memory_space=pltpu.VMEM)
 
     def dma(*shape):
         return pltpu.SemaphoreType.DMA(shape)
 
     def local_layer(tokens, ln_scale, w_in, mlp_bias, q_scale, k_scale, w_out, attn_out_bias, mlp_out_bias):
         tok = tokens.reshape(-1, WID)
-        row = lambda v: v.astype(F32).reshape(1, -1)
+        ob = attn_out_bias.astype(F32) + mlp_out_bias.astype(F32)
+        vec = jnp.concatenate([v.astype(F32) for v in (ln_scale, mlp_bias, q_scale, k_scale)] + [ob]).reshape(1, -1)
         of = lambda *shape: jax.ShapeDtypeStruct(shape, BF16)
-        shapes = [of(*tok.shape), of(ROWS, WID), of(3, WID, NJ * TN), of(4, WID, NJ * TN), of(3, JB, WID), of(4, JB, WID),
+        shapes = [of(*tok.shape), of((NK - NL) * HALF, TN), of(ROWS, WID), of(3, WID, NJ * TN), of(4, WID, NJ * TN), of(3, JB, WID), of(4, JB, WID),
                   of(3, NS, ROWS, TN), of(ROWS, NS * JB), of(ROWS, WID), of(ROWS, WID), of(ROWS, WID)]
         flops = 2 * ROWS * (2 * WID * NT * TN + NS * JB * 2 * WID)
         pairs = [(8,), (7, NJ), (3, NN, 2), (4, NN), (GROUPS, NN), (2 * GROUPS, NN), (2, 2 * GROUPS, NN), (4,)]
         res = pl.pallas_call(
             kernel,
             out_shape=shapes,
-            in_specs=[hbm, hbm, hbm, hbm, hbm, hbm, hbm, vmem],
+            in_specs=[hbm] * 4,
             out_specs=[hbm] * len(shapes),
             scratch_shapes=[
                 pltpu.VMEM((2, M, KH), BF16),
@@ -674,13 +717,37 @@
                 pltpu.VMEM((2, 1, WID), F32),
                 pltpu.VMEM((NS, 1, UNITS // 2), F32),
                 pltpu.VMEM((2, 1, DH), F32),
-                dma(2, 2), dma(2, 5), dma(2), dma(2), dma(2, 3), dma(2, 4), dma(2, 2), dma(4),
+                pltpu.VMEM((1, WID), F32),
+                dma(2, 2), dma(2, 5), dma(2), dma(2), dma(2, 3), dma(2, 5), dma(2, 2), dma(5),
             ] + [dma(*shape) for shape in pairs for _ in range(2)],
             compiler_params=pltpu.CompilerParams(collective_id=0, has_side_effects=True, vmem_limit_bytes=63 * 2**20),
             cost_estimate=pl.CostEstimate(flops=flops, bytes_accessed=2**30, transcendentals=0),
             name="layer",
-        )(tok, row(ln_scale), w_in, row(mlp_bias), row(q_scale), row(k_scale), w_out, row(attn_out_bias) + row(mlp_out_bias))
-        return res[0].reshape(tokens.shape)
+        )(tok, w_in, w_out, vec)
+        base, own = res[0], res[1]
+        far = lax.ppermute(own, 'mx', [(0, 2), (1, 3), (2, 0), (3, 1)])
+        base = pl.pallas_call(
+            copy_kernel,
+            out_shape=of(*tok.shape),
+            in_specs=[hbm],
+            out_specs=hbm,
+            scratch_shapes=[pltpu.VMEM((16, HALF, WID), BF16), dma(2, 16)],
+            compiler_params=pltpu.CompilerParams(vmem_limit_bytes=40 * 2**20),
+            cost_estimate=pl.CostEstimate(flops=2 * 10**10, bytes_accessed=4 * tok.size, transcendentals=0),
+            name="place",
+        )(base)
+        far, base = lax.optimization_barrier((far, base))
+        farther = lax.ppermute(far, 'mx', [(0, 1), (1, 0), (2, 3), (3, 2)])
+        out = pl.pallas_call(
+            tail_kernel,
+            out_shape=of(*tok.shape),
+            in_specs=[hbm] * 3,
+            out_specs=hbm,
+            input_output_aliases={0: 0},
+            scratch_shapes=[pltpu.VMEM((2, (NK - NL) * HALF, TN), BF16), dma(2, 2)],
+            name="place_last",
+        )(base, far, farther)
+        return out.reshape(tokens.shape)
 
     specs_in = (P('dp', None, 'my'), P('my'), P('my', 'mx'), P('mx'), P(), P(), P('mx', 'my'), P('my'), P('my'))
     return jax.shard_map(local_layer, mesh=mesh, in_specs=specs_in, out_specs=P('dp', None, 'my'), check_vma=False)

time: 1550 us -> 1470 us (0.948)
  local copies, waits for them, and re-layouts: 44.1 us -> 0.64 us
  Pallas kernels: 1500 us -> 1460 us
    pallas_call x1 -> x3, Pallas kernels: 1500 us -> 1460 us  [the longest x1 1410 us: local_layer(): pl.pallas_call(kernel, out_shape=shapes, in_specs=[hbm] * 4, out_specs=[h...]
    unnamed x1 -> x2, local copies, waits for them, and re-layouts: 44.1 us -> 0.01 us
  transfers between devices with their start and end apart: 0 -> 2, of which waited for: 0 -> 2; matrix products, arithmetic and copies ran while one was open for 0% -> 0% of each run, Pallas kernels for 0% -> 3%
where the time goes in v3:
time: 1470 us
  Pallas kernels  1460 us (99%)
    pallas_call x1, Pallas kernels, local_layer(): pl.pallas_call(kernel, out_shape=shapes, in_specs=[hbm] * 4, out_specs=[h...  1410 us
    pallas_call x1, Pallas kernels, local_layer(): pl.pallas_call(copy_kernel, out_shape=of(*tok.shape), in_specs=[hbm], out...  41.6 us
  transfers between devices with their start and end apart: 2, of which 2 were waited for; matrix products, arithmetic and copies ran while one was open for 0% of the time, Pallas kernels for 3%

profile of v3, /device:TPU:0, one launch (start us, length us, event | category | flops | bytes accessed | tf_op | source)
XLA Modules:
  0.0 1471.5 jit_solution(2941966400233591287)
XLA Ops:
  0.0 0.7 convert_dynamic-update-slice_fusion.1
  0.7 0.7 convert_dynamic-update-slice_fusion
  1.4 0.7 constant_dynamic-update-slice_fusion.1
  2.0 0.7 constant_dynamic-update-slice_fusion
  2.7 0.7 add_dynamic-update-slice_fusion
  3.4 0.6 reshape.10.vec
  4.1 1411.6 %layer.1 = (bf16[16384,2048]{1,0:T(8,128)(2,1)}, bf16[2048,512]{1,0:T(8,128)(2,1)}, bf16[4096,2048]{1,0:T(8,128)(2,1)}, bf16[3,2048,3584]{2,1,0:T(8,128)(2,1)}, ...) custom-call(bf16[16384,2048]{1,0:T(8,128)(2,1)} %bitcast.tok, ...), custom_call_target="tpu_custom_call" | custom-call | flops 824633720832 | bytes 1073741824 | tf_op jit(solution)/shard_map/layer/pallas_call | solution.py:704
  1415.7 1.4 collective-permute-start
  1417.1 41.6 %place.1.base = bf16[16384,2048]{1,0:T(8,128)(2,1)} custom-call(bf16[16384,2048]{1,0:T(8,128)(2,1)} %get-tuple-element.10.src), custom_call_target="tpu_custom_call" | custom-call | flops 20000000000 | bytes 134217728 | tf_op jit(solution)/shard_map/place/pallas_call | solution.py:729
  1458.7 4.8 collective-permute-done.far
  1463.6 0.0 copy-start
  1463.6 0.0 collective-permute-start.1
  1463.6 4.1 collective-permute-done.1.farther
  1467.7 0.0 copy-done
  1467.7 3.6 place_last.1
Async XLA Ops:
  1415.7 47.9 %collective-permute-start = (bf16[2048,512]{1,0:T(8,128)(2,1)}, bf16[2048,512]{1,0:T(8,128)(2,1)S(1)}, u32[]{:S(2)}, u32[]{:S(2)}) collective-permute-start(bf16[2048,512]{1,0:T(8,128)(2,1)} %get-tuple-element.9), channel_id=1, source_target_pairs={{0,2},{1,3},{2,0},{3,1},{4,6},{5,7},{6,4},{7,5}} | collective-permute-start | bytes 6291464 | tf_op jit(solution)/shard_map/ppermute | solution.py:728
  1463.6 4.1 copy-start
  1463.6 4.1 collective-permute-start.1

commit v4 on v3

--- a/solution.py
+++ b/solution.py
@@ -20,6 +20,7 @@
 NN = WID // TN
 JB = 5 * TN
 KH = 2 * JB
+VEC = 3 * WID + UNITS + 2 * DH
 LN = 128
 EPS = 1e-6
 NK = 2 * GROUPS
@@ -98,15 +99,15 @@
 
     def t_dir(k):
         src = tok.at[pl.ds(pl.multiple_of(row0 + k * HALF, HALF), HALF)]
-        return remote(src, toth.at[pl.ds(pl.multiple_of(k * HALF, HALF), HALF)], t_s.at[k], t_r.at[k], dev_y)
+        return remote(src, toth.at[pl.ds(pl.multiple_of(k * HALF, HALF), HALF)], t_s, t_r.at[k], dev_y)
 
     C, B, D, E, F, G, H = range(7)
 
     def w_own(kind, j, side, dst, dev):
-        return remote(w_in.at[:, in_col(j, side)], dst.at[:, tile(j)], w_s.at[kind, j], w_r.at[kind, j], dev)
+        return remote(w_in.at[:, in_col(j, side)], dst.at[:, tile(j)], w_s.at[kind], w_r.at[kind, j], dev)
 
     def w_pass(kind, j, src, dst, dev):
-        return remote(src.at[:, tile(j)], dst.at[:, tile(j)], w_s.at[kind, j], w_r.at[kind, j], dev)
+        return remote(src.at[:, tile(j)], dst.at[:, tile(j)], w_s.at[kind], w_r.at[kind, j], dev)
 
     tops = [None] + [w1t.at[i] for i in range(NS - 1)]
     bots = [w1b.at[i] for i in range(NS)]
@@ -121,22 +122,18 @@
 
     class Two:
         def __init__(self, kind, n, side, dst, dev):
-            self.copies = [remote(w_out.at[out_row(p, side), tile(n)], dst.at[rows, tile(n)], e_s.at[kind, n, p], e_r.at[kind, n, p], dev)
+            self.copies = [remote(w_out.at[out_row(p, side), tile(n)], dst.at[rows, tile(n)], e_s.at[kind], e_r.at[kind, n], dev)
                            for p, rows in enumerate(PART_ROWS)]
+            self.both = remote(dst.at[:, tile(n)], dst.at[:, tile(n)], e_s.at[kind], e_r.at[kind, n], dev)
 
         def start(self):
             start_all(self.copies)
 
-        def wait_send(self):
-            for one in self.copies:
-                one.wait_send()
-
         def wait_recv(self):
-            for one in self.copies:
-                one.wait_recv()
+            self.both.wait_recv()
 
     def v_pass(kind, n, src, dst, dev):
-        return remote(src.at[:, tile(n)], dst.at[:, tile(n)], d_s.at[kind, n], d_r.at[kind, n], dev)
+        return remote(src.at[:, tile(n)], dst.at[:, tile(n)], d_s.at[kind], d_r.at[kind, n], dev)
 
     mine = [None] + [w2y.at[i] for i in range(NS - 1)]
     theirs = [w2n.at[i] for i in range(NS)]
@@ -149,7 +146,7 @@
     v_h = lambda n: v_pass(E, n, theirs[FAR], theirs[FAR_CORE], dev_c)
 
     def o_y(g, n):
-        return remote(pb.at[rows_of(g), tile(n)], ry.at[rows_of(g), tile(n)], y_s.at[g, n], y_r.at[g, n], dev_y)
+        return remote(pb.at[rows_of(g), tile(n)], ry.at[rows_of(g), tile(n)], y_s, y_r.at[g, n], dev_y)
 
     def part_rows(k):
         return pl.ds(pl.multiple_of(k * HALF, HALF), HALF)
@@ -159,15 +156,15 @@
 
     def o_x(k, n):
         at = out.at[own_out(k), tile(n)]
-        return remote(at, at, x_s.at[k, n], x_r.at[k, n], dev_x)
+        return remote(at, at, x_s, x_r.at[k, n], dev_x)
 
     def o_c(k, n):
         at = out.at[own_out(k), tile(n)]
-        return remote(at, at, o_s.at[0, k, n], o_r.at[0, k, n], dev_c)
+        return remote(at, at, o_s.at[0], o_r.at[0], dev_c)
 
     def o_f(k, n):
         at = out.at[pl.ds(pl.multiple_of(row0_x + k * HALF, HALF), HALF), tile(n)]
-        return remote(at, at, o_s.at[1, k, n], o_r.at[1, k, n], dev_c)
+        return remote(at, at, o_s.at[1], o_r.at[1], dev_c)
 
     lns = vec.at[:, pl.ds(0, WID)]
     my_units = vec.at[:, pl.ds(pl.multiple_of(WID + y * (UNITS // 2), UNITS // 2), UNITS // 2)]
@@ -176,14 +173,16 @@
         (lns, sc.at[1], dev_y), (my_units, ub.at[CORE], dev_c), (my_units, ub.at[FAR], dev_x), (my_units, ub.at[FAR_CORE], dev_d)))]
     small = [pltpu.make_async_copy(src, dst, csem.at[i]) for i, (src, dst) in enumerate((
         (lns, sc.at[0]), (my_units, ub.at[OWN]), (vec.at[:, pl.ds(at, DH)], gains.at[0]),
-        (vec.at[:, pl.ds(at + DH, DH)], gains.at[1]), (vec.at[:, pl.ds(at + 2 * DH, WID)], ob)))]
-
+        (vec.at[:, pl.ds(at + DH, DH)], gains.at[1]), (vec.at[:, pl.ds(at + 2 * DH, WID)], ob.at[0]),
+        (vec.at[:, pl.ds(at + 2 * DH + WID, WID)], ob.at[1])))]
+
+    loop(0, NS, lambda j: w_e(j).start())
     start_all(small_far)
-    loop(0, 4, lambda k: t_dir(k).start())
+    loop(0, NS, lambda k: t_dir(k).start())
     loop(0, NJ, lambda j: w_c(j).start())
-    loop(4, 8, lambda k: t_dir(k).start())
+    loop(NS, NK, lambda k: t_dir(k).start())
     loop(0, NN, lambda n: v_c(n).start())
-    loop(0, 5, lambda j: w_e(j).start())
+    w_e(NS).start()
     loop(0, NJ, lambda j: w_b(j).start())
     loop(0, NN, lambda n: v_b(n).start())
     start_all(small)
@@ -502,7 +501,7 @@
 
     def fin_do(k, n, e):
         wait_all(fin_loads(k, n, e))
-        total = sv[e, 0].astype(F32) + sv[e, 1].astype(F32) + ob[:, tile(n)] + sv[e, 2].astype(F32)
+        total = sv[e, 0].astype(F32) + sv[e, 1].astype(F32) + (ob[0, :, tile(n)] + ob[1, :, tile(n)]) + sv[e, 2].astype(F32)
         sv[e, 3] = total.astype(BF16)
         fin_store(k, n, e).start()
 
@@ -618,30 +617,28 @@
 
     loop(STEPS, STEPS + 6, service)
     loop(0, NK, lambda k: hand_out(k, 2))
-    loop(0, NK - NL, lambda k: hand_out(k, 3))
 
     for one in small_far:
         one.wait_send()
-    loop(0, 8, lambda k: t_dir(k).wait_send())
-    for one in (w_c, w_b, w_d, w_e, w_f, w_g, w_h):
-        loop(0, NJ, lambda j, one=one: one(j).wait_send())
-    for one in (v_c, v_b, v_e, v_d, v_f, v_g, v_h):
-        loop(0, NN, lambda n, one=one: one(n).wait_send())
-
-    def settle(n):
-        loop(0, GROUPS, lambda g: o_y(g, n).wait_send())
-
-        def chunk(k):
-            o_c(k, n).wait_send()
-            o_c(k, n).wait_recv()
-        loop(0, NK, chunk)
-
-        def far_chunk(k):
-            o_x(k, n).wait_send()
-            o_f(k, n).wait_send()
-            o_f(k, n).wait_recv()
-        loop(0, NK - NL * (n // (NN - 1)), far_chunk)
-    loop(0, NN, settle)
+    remote(toth, toth, t_s, t_s, dev_y).wait_send()
+    for kind in range(C + NJ):
+        remote(bots[OWN], bots[OWN], w_s.at[kind], w_s.at[kind], dev_y).wait_send()
+    for kind in range(NS):
+        remote(theirs[OWN], theirs[OWN], d_s.at[kind], d_s.at[kind], dev_y).wait_send()
+    for kind in range(NS - 1):
+        remote(theirs[OWN], theirs[OWN], e_s.at[kind], e_s.at[kind], dev_y).wait_send()
+    remote(pb, pb, y_s, y_s, dev_y).wait_send()
+    mine_out = out.at[pl.ds(pl.multiple_of(row0, ROWS), ROWS)]
+    near_out = remote(mine_out, mine_out, o_s.at[0], o_r.at[0], dev_c)
+    near_out.wait_send()
+    near_out.wait_recv()
+
+    loop(0, NK - NL, lambda k: hand_out(k, NN - 1))
+    sent = out.at[pl.ds(pl.multiple_of(row0, ROWS), ROWS - (NK - NL) * HALF // NN)]
+    remote(sent, sent, x_s, x_s, dev_x).wait_send()
+    far_out = remote(sent, sent, o_s.at[1], o_r.at[1], dev_c)
+    far_out.wait_send()
+    far_out.wait_recv()
 
 
 def copy_kernel(src, dst, buf, sem):
@@ -673,17 +670,16 @@
 def tail_kernel(base, far, farther, out, buf, sem):
     mi = lax.axis_index("mx")
     x, c = mi // 2, mi % 2
-    pieces = ((far, c), (farther, 1 - c))
-    loads = [pltpu.make_async_copy(ref, buf.at[i], sem.at[0, i]) for i, (ref, _) in enumerate(pieces)]
-    start_all(loads)
-    stores = []
-    for i, (_, cc) in enumerate(pieces):
+    moves = []
+    for i, (ref, cc) in enumerate(((far, c), (farther, 1 - c))):
         at = pl.multiple_of((2 * (1 - x) + cc) * ROWS + NL * HALF, HALF)
-        store = pltpu.make_async_copy(buf.at[i], out.at[pl.ds(at, (NK - NL) * HALF), pl.ds((NN - 1) * TN, TN)], sem.at[1, i])
-        loads[i].wait()
+        to = out.at[pl.ds(at, (NK - NL) * HALF), pl.ds((NN - 1) * TN, TN)]
+        moves.append((pltpu.make_async_copy(ref, buf.at[i], sem.at[0, i]), pltpu.make_async_copy(buf.at[i], to, sem.at[1, i])))
+    start_all(load for load, _ in moves)
+    for load, store in moves:
+        load.wait()
         store.start()
-        stores.append(store)
-    wait_all(stores)
+    wait_all(store for _, store in moves)
 
 
 def solution(mesh):
@@ -694,13 +690,16 @@
 
     def local_layer(tokens, ln_scale, w_in, mlp_bias, q_scale, k_scale, w_out, attn_out_bias, mlp_out_bias):
         tok = tokens.reshape(-1, WID)
-        ob = attn_out_bias.astype(F32) + mlp_out_bias.astype(F32)
-        vec = jnp.concatenate([v.astype(F32) for v in (ln_scale, mlp_bias, q_scale, k_scale)] + [ob]).reshape(1, -1)
+        vec, at = None, 0
+        for v in (ln_scale, mlp_bias, q_scale, k_scale, attn_out_bias, mlp_out_bias):
+            wide = jnp.pad(v.astype(F32), (at, VEC - at - v.size), constant_values=-jnp.inf)
+            vec = wide if vec is None else jnp.maximum(vec, wide)
+            at += v.size
         of = lambda *shape: jax.ShapeDtypeStruct(shape, BF16)
         shapes = [of(*tok.shape), of((NK - NL) * HALF, TN), of(ROWS, WID), of(3, WID, NJ * TN), of(4, WID, NJ * TN), of(3, JB, WID), of(4, JB, WID),
                   of(3, NS, ROWS, TN), of(ROWS, NS * JB), of(ROWS, WID), of(ROWS, WID), of(ROWS, WID)]
         flops = 2 * ROWS * (2 * WID * NT * TN + NS * JB * 2 * WID)
-        pairs = [(8,), (7, NJ), (3, NN, 2), (4, NN), (GROUPS, NN), (2 * GROUPS, NN), (2, 2 * GROUPS, NN), (4,)]
+        pairs = [(), (NK,), (7,), (7, NJ), (3,), (3, NN), (NS,), (NS, NN), (), (GROUPS, NN), (), (NK, NN), (2,), (2,), (NS,), (NS,)]
         res = pl.pallas_call(
             kernel,
             out_shape=shapes,
@@ -717,13 +716,13 @@
                 pltpu.VMEM((2, 1, WID), F32),
                 pltpu.VMEM((NS, 1, UNITS // 2), F32),
                 pltpu.VMEM((2, 1, DH), F32),
-                pltpu.VMEM((1, WID), F32),
-                dma(2, 2), dma(2, 5), dma(2), dma(2), dma(2, 3), dma(2, 5), dma(2, 2), dma(5),
-            ] + [dma(*shape) for shape in pairs for _ in range(2)],
+                pltpu.VMEM((2, 1, WID), F32),
+                dma(2, 2), dma(2, 5), dma(2), dma(2), dma(2, 3), dma(2, 5), dma(2, 2), dma(6),
+            ] + [dma(*shape) for shape in pairs],
             compiler_params=pltpu.CompilerParams(collective_id=0, has_side_effects=True, vmem_limit_bytes=63 * 2**20),
             cost_estimate=pl.CostEstimate(flops=flops, bytes_accessed=2**30, transcendentals=0),
             name="layer",
-        )(tok, w_in, w_out, vec)
+        )(tok, w_in, w_out, vec.reshape(1, VEC))
         base, own = res[0], res[1]
         far = lax.ppermute(own, 'mx', [(0, 2), (1, 3), (2, 0), (3, 1)])
         base = pl.pallas_call(

time: 1470 us -> 1470 us (level)
  no operation moved by 1% of the time
where the time goes in v4:
time: 1470 us
  Pallas kernels  1450 us (99%)
    pallas_call x1, Pallas kernels, local_layer(): pl.pallas_call(kernel, out_shape=shapes, in_specs=[hbm] * 4, out_specs=[h...  1410 us
    pallas_call x1, Pallas kernels, local_layer(): pl.pallas_call(copy_kernel, out_shape=of(*tok.shape), in_specs=[hbm], out...  41.6 us
  transfers between devices with their start and end apart: 2, of which 2 were waited for; matrix products, arithmetic and copies ran while one was open for 0% of the time, Pallas kernels for 3%

profile of v4, /device:TPU:0, one launch (start us, length us, event | category | flops | bytes accessed | tf_op | source)
XLA Modules:
  0.0 1466.3 jit_solution(8155929181593190583)
XLA Ops:
  0.0 0.8 convert_maximum_fusion
  0.8 0.6 reshape.10.vec
  1.4 1409.1 %layer.1 = (bf16[16384,2048]{1,0:T(8,128)(2,1)}, bf16[2048,512]{1,0:T(8,128)(2,1)}, bf16[4096,2048]{1,0:T(8,128)(2,1)}, bf16[3,2048,3584]{2,1,0:T(8,128)(2,1)}, ...) custom-call(bf16[16384,2048]{1,0:T(8,128)(2,1)} %bitcast.tok, ...), custom_call_target="tpu_custom_call" | custom-call | flops 824633720832 | bytes 1073741824 | tf_op jit(solution)/shard_map/layer/pallas_call | solution.py:703
  1410.5 1.5 collective-permute-start
  1412.1 41.6 %place.1.base = bf16[16384,2048]{1,0:T(8,128)(2,1)} custom-call(bf16[16384,2048]{1,0:T(8,128)(2,1)} %get-tuple-element.10.src), custom_call_target="tpu_custom_call" | custom-call | flops 20000000000 | bytes 134217728 | tf_op jit(solution)/shard_map/place/pallas_call | solution.py:728
  1453.7 4.7 collective-permute-done.far
  1458.4 0.0 copy-start
  1458.4 0.0 collective-permute-start.1
  1458.4 4.1 collective-permute-done.1.farther
  1462.5 0.0 copy-done
  1462.5 3.6 place_last.1
Async XLA Ops:
  1410.5 47.9 %collective-permute-start = (bf16[2048,512]{1,0:T(8,128)(2,1)}, bf16[2048,512]{1,0:T(8,128)(2,1)S(1)}, u32[]{:S(2)}, u32[]{:S(2)}) collective-permute-start(bf16[2048,512]{1,0:T(8,128)(2,1)} %get-tuple-element.9), channel_id=1, source_target_pairs={{0,2},{1,3},{2,0},{3,1},{4,6},{5,7},{6,4},{7,5}} | collective-permute-start | bytes 6291464 | tf_op jit(solution)/shard_map/ppermute | solution.py:727
  1458.4 4.1 copy-start
  1458.4 4.1 collective-permute-start.1

commit v5 on v4

--- a/solution.py
+++ b/solution.py
@@ -1,3 +1,5 @@
+import functools
+
 import jax
 import jax.numpy as jnp
 from jax import lax
@@ -183,6 +185,7 @@
     loop(NS, NK, lambda k: t_dir(k).start())
     loop(0, NN, lambda n: v_c(n).start())
     w_e(NS).start()
+    w_e(NS + 1).start()
     loop(0, NJ, lambda j: w_b(j).start())
     loop(0, NN, lambda n: v_b(n).start())
     start_all(small)
@@ -246,9 +249,9 @@
                 w_d(j).start()
                 w_f(j).start()
 
-                @pl.when((j == 1) | (j == 3))
+                @pl.when(j == 2)
                 def _():
-                    w_e((j + 9) // 2).start()
+                    w_e(NJ - 1).start()
 
                 @pl.when(j == NJ - 1)
                 def _():
@@ -528,7 +531,7 @@
     STEPS = 2 * NN * NK
 
     def service(v):
-        f = v - 12
+        f = v - 11
         n, i = f // 16, f % 16
 
         @pl.when((f >= 0) & (i >= 2) & (i < NK + 2))
@@ -598,6 +601,10 @@
             j_copy(v + 1).start()
             j_copy(v).wait()
             acc[...] = jnp.dot(zj[0], wbuf[w2_slot(m, 0)], preferred_element_type=F32)
+
+            @pl.when(g > 0)
+            def _():
+                p_finish(m, g - 1)
             service(v)
 
             @pl.when(v + 2 < STEPS)
@@ -606,16 +613,12 @@
             j_copy(v + 1).wait()
             ptile[g % 2] = (acc[...] + jnp.dot(zj[1], wbuf[w2_slot(m, 1)], preferred_element_type=F32)).astype(BF16)
             p_start(m, g)
-
-            @pl.when(g > 0)
-            def _():
-                p_finish(m, g - 1)
             service(v + 1)
         loop(0, GROUPS, one)
         p_finish(m, GROUPS - 1)
     loop(0, 2 * NN, w2_tile)
 
-    loop(STEPS, STEPS + 6, service)
+    loop(STEPS, STEPS + 5, service)
     loop(0, NK, lambda k: hand_out(k, 2))
 
     for one in small_far:
@@ -667,14 +670,16 @@
         every[i][1].wait()
 
 
-def tail_kernel(base, far, farther, out, buf, sem):
+def tail_kernel(other, base, src, out, buf, sem):
     mi = lax.axis_index("mx")
-    x, c = mi // 2, mi % 2
+    x, c = mi // 2, (mi + other) % 2
+    at = pl.multiple_of((2 * (1 - x) + c) * ROWS + NL * HALF, HALF)
+    rows = (NK - NL) * HALF // NN
     moves = []
-    for i, (ref, cc) in enumerate(((far, c), (farther, 1 - c))):
-        at = pl.multiple_of((2 * (1 - x) + cc) * ROWS + NL * HALF, HALF)
-        to = out.at[pl.ds(at, (NK - NL) * HALF), pl.ds((NN - 1) * TN, TN)]
-        moves.append((pltpu.make_async_copy(ref, buf.at[i], sem.at[0, i]), pltpu.make_async_copy(buf.at[i], to, sem.at[1, i])))
+    for i in range(NN):
+        to = out.at[pl.ds(at + i * rows, rows), pl.ds((NN - 1) * TN, TN)]
+        part = buf.at[pl.ds(i * rows, rows)]
+        moves.append((pltpu.make_async_copy(src.at[pl.ds(i * rows, rows)], part, sem.at[0, i]), pltpu.make_async_copy(part, to, sem.at[1, i])))
     start_all(load for load, _ in moves)
     for load, store in moves:
         load.wait()
@@ -737,16 +742,18 @@
         )(base)
         far, base = lax.optimization_barrier((far, base))
         farther = lax.ppermute(far, 'mx', [(0, 1), (1, 0), (2, 3), (3, 2)])
-        out = pl.pallas_call(
-            tail_kernel,
-            out_shape=of(*tok.shape),
-            in_specs=[hbm] * 3,
-            out_specs=hbm,
-            input_output_aliases={0: 0},
-            scratch_shapes=[pltpu.VMEM((2, (NK - NL) * HALF, TN), BF16), dma(2, 2)],
-            name="place_last",
-        )(base, far, farther)
-        return out.reshape(tokens.shape)
+        for other, piece in enumerate((far, farther)):
+            base = pl.pallas_call(
+                functools.partial(tail_kernel, other),
+                out_shape=of(*tok.shape),
+                in_specs=[hbm] * 2,
+                out_specs=hbm,
+                input_output_aliases={0: 0},
+                scratch_shapes=[pltpu.VMEM(((NK - NL) * HALF, TN), BF16), dma(2, NN)],
+                cost_estimate=pl.CostEstimate(flops=10**9, bytes_accessed=4 * piece.size, transcendentals=0),
+                name="place_last",
+            )(base, piece)
+        return base.reshape(tokens.shape)
 
     specs_in = (P('dp', None, 'my'), P('my'), P('my', 'mx'), P('mx'), P(), P(), P('mx', 'my'), P('my'), P('my'))
     return jax.shard_map(local_layer, mesh=mesh, in_specs=specs_in, out_specs=P('dp', None, 'my'), check_vma=False)

time: 1470 us -> 1460 us (level)
  no operation moved by 1% of the time
where the time goes in v5:
time: 1460 us
  Pallas kernels  1450 us (99%)
    pallas_call x1, Pallas kernels, local_layer(): pl.pallas_call(kernel, out_shape=shapes, in_specs=[hbm] * 4, out_specs=[h...  1400 us
    pallas_call x1, Pallas kernels, local_layer(): pl.pallas_call(copy_kernel, out_shape=of(*tok.shape), in_specs=[hbm], out...  41.6 us
  transfers between devices with their start and end apart: 2, of which 2 were waited for; matrix products, arithmetic and copies ran while one was open for 0% of the time, Pallas kernels for 3%

profile of v5, /device:TPU:0, one launch (start us, length us, event | category | flops | bytes accessed | tf_op | source)
XLA Modules:
  0.0 1460.2 jit_solution(9652608542032353509)
XLA Ops:
  0.0 0.8 convert_maximum_fusion
  0.8 0.6 reshape.10.vec
  1.4 1404.2 %layer.1 = (bf16[16384,2048]{1,0:T(8,128)(2,1)}, bf16[2048,512]{1,0:T(8,128)(2,1)}, bf16[4096,2048]{1,0:T(8,128)(2,1)}, bf16[3,2048,3584]{2,1,0:T(8,128)(2,1)}, ...) custom-call(bf16[16384,2048]{1,0:T(8,128)(2,1)} %bitcast.tok, ...), custom_call_target="tpu_custom_call" | custom-call | flops 824633720832 | bytes 1073741824 | tf_op jit(solution)/shard_map/layer/pallas_call | solution.py:708
  1405.7 1.5 collective-permute-start
  1407.2 41.6 %place.1.base = bf16[16384,2048]{1,0:T(8,128)(2,1)} custom-call(bf16[16384,2048]{1,0:T(8,128)(2,1)} %get-tuple-element.10.src), custom_call_target="tpu_custom_call" | custom-call | flops 20000000000 | bytes 134217728 | tf_op jit(solution)/shard_map/place/pallas_call | solution.py:733
  1448.8 4.7 collective-permute-done.src
  1453.5 0.0 copy-start
  1453.5 0.0 collective-permute-start.1
  1453.5 1.3 copy-done
  1454.9 2.4 place_last.2.base
  1457.3 0.3 collective-permute-done.1.src
  1457.6 2.4 place_last.3
Async XLA Ops:
  1405.7 47.9 %collective-permute-start = (bf16[2048,512]{1,0:T(8,128)(2,1)}, bf16[2048,512]{1,0:T(8,128)(2,1)S(1)}, u32[]{:S(2)}, u32[]{:S(2)}) collective-permute-start(bf16[2048,512]{1,0:T(8,128)(2,1)} %get-tuple-element.9), channel_id=1, source_target_pairs={{0,2},{1,3},{2,0},{3,1},{4,6},{5,7},{6,4},{7,5}} | collective-permute-start | bytes 6291464 | tf_op jit(solution)/shard_map/ppermute | solution.py:732
  1453.5 1.3 copy-start
  1453.5 4.1 collective-permute-start.1

commit v6 on v5

--- a/solution.py
+++ b/solution.py
@@ -22,7 +22,7 @@
 NN = WID // TN
 JB = 5 * TN
 KH = 2 * JB
-VEC = 3 * WID + UNITS + 2 * DH
+LANES = 128
 LN = 128
 EPS = 1e-6
 NK = 2 * GROUPS
@@ -76,9 +76,9 @@
         one.wait()
 
 
-def kernel(tok, w_in, w_out, vec,
+def kernel(tok, w_in, w_out, lns, mb, qs, ks, ab, bb,
            out, tail, toth, w1t, w1b, w2y, w2n, qkv, jb, pa, pb, ry,
-           zj, wbuf, ptile, acc, abuf, sv, lbuf, sc, ub, gains, ob,
+           zj, wbuf, ptile, acc, abuf, sv, lbuf, sc, ub, gains, ob, raw, raw2,
            w1sem, w2sem, jsem, psem, asem, vsem, lsem, csem,
            t_s, t_r, w_s, w_r, e_s, e_r, d_s, d_r, y_s, y_r, x_s, x_r, o_s, o_r, m_s, m_r):
     y = lax.axis_index("my")
@@ -168,15 +168,17 @@
         at = out.at[pl.ds(pl.multiple_of(row0_x + k * HALF, HALF), HALF), tile(n)]
         return remote(at, at, o_s.at[1], o_r.at[1], dev_c)
 
-    lns = vec.at[:, pl.ds(0, WID)]
-    my_units = vec.at[:, pl.ds(pl.multiple_of(WID + y * (UNITS // 2), UNITS // 2), UNITS // 2)]
-    at = WID + UNITS
-    small_far = [remote(src, dst, m_s.at[i], m_r.at[i], dev) for i, (src, dst, dev) in enumerate((
-        (lns, sc.at[1], dev_y), (my_units, ub.at[CORE], dev_c), (my_units, ub.at[FAR], dev_x), (my_units, ub.at[FAR_CORE], dev_d)))]
+    rows = WID // LANES
+    few = DH // LANES
+    my_units = mb.at[pl.ds(pl.multiple_of(y * rows, rows), rows)]
+    small_far = [remote(src, raw.at[i], m_s.at[i], m_r.at[i], dev) for i, (src, dev) in enumerate((
+        (lns, dev_y), (my_units, dev_c), (my_units, dev_x), (my_units, dev_d)))]
     small = [pltpu.make_async_copy(src, dst, csem.at[i]) for i, (src, dst) in enumerate((
-        (lns, sc.at[0]), (my_units, ub.at[OWN]), (vec.at[:, pl.ds(at, DH)], gains.at[0]),
-        (vec.at[:, pl.ds(at + DH, DH)], gains.at[1]), (vec.at[:, pl.ds(at + 2 * DH, WID)], ob.at[0]),
-        (vec.at[:, pl.ds(at + 2 * DH + WID, WID)], ob.at[1])))]
+        (lns, raw.at[NS]), (my_units, raw.at[NS + 1]), (ab, raw.at[NS + 2]), (bb, raw.at[NS + 3]), (qs, raw2.at[0]), (ks, raw2.at[1])))]
+
+    def spread(src, dst, count):
+        for i in range(count):
+            dst[:, i * LANES:(i + 1) * LANES] = src[i:i + 1].astype(F32)
 
     loop(0, NS, lambda j: w_e(j).start())
     start_all(small_far)
@@ -192,6 +194,10 @@
     wait_all(small)
     for one in small_far:
         one.wait_recv()
+    for i, dst in enumerate((sc.at[1], ub.at[CORE], ub.at[FAR], ub.at[FAR_CORE], sc.at[0], ub.at[OWN], ob.at[0], ob.at[1])):
+        spread(raw.at[i], dst, rows)
+    for i in range(2):
+        spread(raw2.at[i], gains.at[i], few)
 
     def l_copies(g, i, slot):
         at = pl.multiple_of(g * M + i * LN, LN)
@@ -695,11 +701,7 @@
 
     def local_layer(tokens, ln_scale, w_in, mlp_bias, q_scale, k_scale, w_out, attn_out_bias, mlp_out_bias):
         tok = tokens.reshape(-1, WID)
-        vec, at = None, 0
-        for v in (ln_scale, mlp_bias, q_scale, k_scale, attn_out_bias, mlp_out_bias):
-            wide = jnp.pad(v.astype(F32), (at, VEC - at - v.size), constant_values=-jnp.inf)
-            vec = wide if vec is None else jnp.maximum(vec, wide)
-            at += v.size
+        vecs = [v.reshape(-1, LANES) for v in (ln_scale, mlp_bias, q_scale, k_scale, attn_out_bias, mlp_out_bias)]
         of = lambda *shape: jax.ShapeDtypeStruct(shape, BF16)
         shapes = [of(*tok.shape), of((NK - NL) * HALF, TN), of(ROWS, WID), of(3, WID, NJ * TN), of(4, WID, NJ * TN), of(3, JB, WID), of(4, JB, WID),
                   of(3, NS, ROWS, TN), of(ROWS, NS * JB), of(ROWS, WID), of(ROWS, WID), of(ROWS, WID)]
@@ -708,7 +710,7 @@
         res = pl.pallas_call(
             kernel,
             out_shape=shapes,
-            in_specs=[hbm] * 4,
+            in_specs=[hbm] * 9,
             out_specs=[hbm] * len(shapes),
             scratch_shapes=[
                 pltpu.VMEM((2, M, KH), BF16),
@@ -722,12 +724,14 @@
                 pltpu.VMEM((NS, 1, UNITS // 2), F32),
                 pltpu.VMEM((2, 1, DH), F32),
                 pltpu.VMEM((2, 1, WID), F32),
+                pltpu.VMEM((2 * NS, WID // LANES, LANES), BF16),
+                pltpu.VMEM((2, DH // LANES, LANES), BF16),
                 dma(2, 2), dma(2, 5), dma(2), dma(2), dma(2, 3), dma(2, 5), dma(2, 2), dma(6),
             ] + [dma(*shape) for shape in pairs],
             compiler_params=pltpu.CompilerParams(collective_id=0, has_side_effects=True, vmem_limit_bytes=63 * 2**20),
             cost_estimate=pl.CostEstimate(flops=flops, bytes_accessed=2**30, transcendentals=0),
             name="layer",
-        )(tok, w_in, w_out, vec.reshape(1, VEC))
+        )(tok, w_in, w_out, *vecs)
         base, own = res[0], res[1]
         far = lax.ppermute(own, 'mx', [(0, 2), (1, 3), (2, 0), (3, 1)])
         base = pl.pallas_call(

time: 1460 us -> 1460 us (level)
  no operation moved by 1% of the time
where the time goes in v6:
time: 1460 us
  Pallas kernels  1450 us (99%)
    pallas_call x1, Pallas kernels, local_layer(): pl.pallas_call(kernel, out_shape=shapes, in_specs=[hbm] * 9, out_specs=[h...  1400 us
    pallas_call x1, Pallas kernels, local_layer(): pl.pallas_call(copy_kernel, out_shape=of(*tok.shape), in_specs=[hbm], out...  41.6 us
  transfers between devices with their start and end apart: 2, of which 2 were waited for; matrix products, arithmetic and copies ran while one was open for 0% of the time, Pallas kernels for 3%

profile of v6, /device:TPU:0, one launch (start us, length us, event | category | flops | bytes accessed | tf_op | source)
XLA Modules:
  0.0 1458.7 jit_solution(14381456075765335273)
XLA Ops:
  0.0 1404.1 %layer.1 = (bf16[16384,2048]{1,0:T(8,128)(2,1)}, bf16[2048,512]{1,0:T(8,128)(2,1)}, bf16[4096,2048]{1,0:T(8,128)(2,1)}, bf16[3,2048,3584]{2,1,0:T(8,128)(2,1)}, ...) custom-call(bf16[16384,2048]{1,0:T(8,128)(2,1)} %bitcast.tok, ...), custom_call_target="tpu_custom_call" | custom-call | flops 824633720832 | bytes 1073741824 | tf_op jit(solution)/shard_map/layer/pallas_call | solution.py:710
  1404.1 1.5 collective-permute-start
  1405.7 41.6 %place.1.base = bf16[16384,2048]{1,0:T(8,128)(2,1)} custom-call(bf16[16384,2048]{1,0:T(8,128)(2,1)} %get-tuple-element.10.src), custom_call_target="tpu_custom_call" | custom-call | flops 20000000000 | bytes 134217728 | tf_op jit(solution)/shard_map/place/pallas_call | solution.py:737
  1447.3 4.7 collective-permute-done.src
  1452.0 0.0 copy-start
  1452.0 0.0 collective-permute-start.1
  1452.0 1.3 copy-done
  1453.3 2.4 place_last.2.base
  1455.8 0.3 collective-permute-done.1.src
  1456.1 2.4 place_last.3
Async XLA Ops:
  1404.1 47.9 %collective-permute-start = (bf16[2048,512]{1,0:T(8,128)(2,1)}, bf16[2048,512]{1,0:T(8,128)(2,1)S(1)}, u32[]{:S(2)}, u32[]{:S(2)}) collective-permute-start(bf16[2048,512]{1,0:T(8,128)(2,1)} %get-tuple-element.9), channel_id=1, source_target_pairs={{0,2},{1,3},{2,0},{3,1},{4,6},{5,7},{6,4},{7,5}} | collective-permute-start | bytes 6291464 | tf_op jit(solution)/shard_map/ppermute | solution.py:736
  1452.0 1.3 copy-start
  1452.0 4.1 collective-permute-start.1

commit v7 on v6

--- a/solution.py
+++ b/solution.py
@@ -6,6 +6,7 @@
 from jax.experimental import pallas as pl
 from jax.experimental.pallas import tpu as pltpu
 from jax.sharding import PartitionSpec as P
+
 
 MESH = pl.DeviceIdType.MESH
 F32, BF16 = jnp.float32, jnp.bfloat16
@@ -27,6 +28,8 @@
 EPS = 1e-6
 NK = 2 * GROUPS
 NL = NK // 2
+TAILS = ((NL, NK - 1), (NK - 1, NK))
+SPLIT = 3 * NK + NL
 
 
 def in_col(j, side):
@@ -63,6 +66,7 @@
     def run(i, carry):
         body(i)
         return carry
+
     lax.fori_loop(lo, hi, run, 0)
 
 
@@ -77,7 +81,7 @@
 
 
 def kernel(tok, w_in, w_out, lns, mb, qs, ks, ab, bb,
-           out, tail, toth, w1t, w1b, w2y, w2n, qkv, jb, pa, pb, ry,
+           out, tail, tail2, toth, w1t, w1b, w2y, w2n, qkv, jb, pa, pb, ry,
            zj, wbuf, ptile, acc, abuf, sv, lbuf, sc, ub, gains, ob, raw, raw2,
            w1sem, w2sem, jsem, psem, asem, vsem, lsem, csem,
            t_s, t_r, w_s, w_r, e_s, e_r, d_s, d_r, y_s, y_r, x_s, x_r, o_s, o_r, m_s, m_r):
@@ -221,6 +225,7 @@
             @pl.when(i + 1 < steps)
             def _():
                 start_all(l_copies(g, i + 1, 1 - slot))
+
             wait_all(l_copies(g, i, slot))
             step = 64
 
@@ -234,7 +239,9 @@
                 to = pl.ds(pl.multiple_of(i * LN + k * step, step), step)
                 zj[g % 2, to, :WID] = (a * inv * sc[0]).astype(BF16)
                 zj[g % 2, to, WID:2 * WID] = (b * inv * sc[1]).astype(BF16)
+
             loop(0, LN // step, part)
+
         loop(0, steps, rows)
 
     def w1_copies(slot, top, bottom):
@@ -337,6 +344,7 @@
             @pl.when(j > 2)
             def _():
                 h_store(gl, jb.at[rows_of(g), pl.ds(pl.multiple_of(s * JB + (j - 2) * TN, TN), TN)]).start()
+
         loop(0, 2, one)
 
     def a_loads(p, w, slot):
@@ -357,6 +365,7 @@
             @pl.when(w + 1 < units)
             def _():
                 start_all(a_loads(p, w + 1, 1 - slot))
+
             wait_all(a_loads(p, w, slot))
 
             @pl.when(w >= 2)
@@ -373,8 +382,10 @@
                         e = jnp.exp(lg - jnp.max(lg, -1, keepdims=True))
                         prob = (e / jnp.sum(e, -1, keepdims=True)).astype(BF16)
                         ptile[slot, at, cols] = jnp.dot(prob, v, preferred_element_type=F32).astype(BF16)
+
             loop(0, M // SEQ // 2, images)
             a_store(p, w, slot).start()
+
         loop(0, units, unit)
         a_store(p, units - 2, 0).wait()
         a_store(p, units - 1, 1).wait()
@@ -470,6 +481,7 @@
             @pl.when(p == 1)
             def _():
                 fetch_next()
+
             w1_tile(p, t)
 
             @pl.when(p == 0)
@@ -481,9 +493,11 @@
                 def _(todo=todo):
                     for one in todo:
                         one()
+
         loop(0, NT, step)
         h_done(0)
         h_done(1)
+
     loop(0, 2, w1_pass)
 
     def load(e, i, src):
@@ -497,7 +511,16 @@
         return pltpu.make_async_copy(sv.at[e, 3], out.at[own_out(k), tile(n)], vsem.at[e, 3])
 
     def tail_store(k, e):
-        return pltpu.make_async_copy(sv.at[e, 3], tail.at[part_rows(k - NL)], vsem.at[e, 4])
+        def to(ref):
+            return pltpu.make_async_copy(sv.at[e, 3], ref, vsem.at[e, 4])
+
+        @pl.when(k < NK - 1)
+        def _():
+            to(tail.at[part_rows(k - NL)]).start()
+
+        @pl.when(k == NK - 1)
+        def _():
+            to(tail2).start()
 
     def is_tail(k, n):
         return (n == NN - 1) & (k >= NL)
@@ -506,6 +529,7 @@
         @pl.when(k % 2 == 0)
         def _():
             o_y(k // 2, n).wait_recv()
+
         start_all(fin_loads(k, n, e))
 
     def fin_do(k, n, e):
@@ -516,18 +540,19 @@
 
         @pl.when(is_tail(k, n))
         def _():
-            tail_store(k, e).start()
+            tail_store(k, e)
 
     def fin_send(k, n, e):
         fin_store(k, n, e).wait()
 
         @pl.when(is_tail(k, n))
         def _():
-            tail_store(k, e).wait()
+            pltpu.make_async_copy(sv.at[e, 3], tail2, vsem.at[e, 4]).wait()
 
         @pl.when(jnp.logical_not(is_tail(k, n)))
         def _():
             o_x(k, n).start()
+
         o_c(k, n).start()
 
     def hand_out(k, n):
@@ -567,7 +592,7 @@
         return n, lambda ref: pltpu.make_async_copy(ptile.at[slot], ref.at[rows_of(g), tile(n)], psem.at[slot])
 
     def p_start(m, g):
-        n, to = p_copy(m, g)
+        _, to = p_copy(m, g)
 
         @pl.when(m % 2 == 0)
         def _():
@@ -600,6 +625,7 @@
         @pl.when(m + 1 < 2 * NN)
         def _():
             fetch2(m + 1)
+
         arrive2(m)
 
         def one(g):
@@ -611,17 +637,21 @@
             @pl.when(g > 0)
             def _():
                 p_finish(m, g - 1)
+
             service(v)
 
             @pl.when(v + 2 < STEPS)
             def _():
                 j_copy(v + 2).start()
+
             j_copy(v + 1).wait()
             ptile[g % 2] = (acc[...] + jnp.dot(zj[1], wbuf[w2_slot(m, 1)], preferred_element_type=F32)).astype(BF16)
             p_start(m, g)
             service(v + 1)
+
         loop(0, GROUPS, one)
         p_finish(m, GROUPS - 1)
+
     loop(0, 2 * NN, w2_tile)
 
     loop(STEPS, STEPS + 5, service)
@@ -650,7 +680,8 @@
     far_out.wait_recv()
 
 
-def copy_kernel(src, dst, buf, sem):
+def copy_kernel(lo, hi, src, *rest):
+    dst, buf, sem = rest[-3:]
     slots = buf.shape[0]
     x = lax.axis_index("mx") // 2
 
@@ -659,38 +690,31 @@
         rows = pl.ds(pl.multiple_of(first * 2 * ROWS + (i % (2 * NK)) * HALF, HALF), HALF)
         late = i >= 2 * NK and i % NK >= NL
         cols = pl.ds(0, WID - TN if late else WID)
-        k = i % slots
+        k = (i - lo) % slots
         return (pltpu.make_async_copy(src.at[rows, cols], buf.at[k, :, cols], sem.at[0, k]),
                 pltpu.make_async_copy(buf.at[k, :, cols], dst.at[rows, cols], sem.at[1, k]))
-    every = [moves(i) for i in range(4 * NK)]
-    ahead = slots // 2
-    for i in range(4 * NK + ahead):
-        if i < 4 * NK:
+
+    every = [moves(i) for i in range(lo, hi)]
+    ahead, count = 12, hi - lo
+    for i in range(count + ahead):
+        if i < count:
             if i >= slots:
                 every[i - slots][1].wait()
             every[i][0].start()
         if i >= ahead:
             every[i - ahead][0].wait()
             every[i - ahead][1].start()
-    for i in range(4 * NK - slots, 4 * NK):
-        every[i][1].wait()
-
-
-def tail_kernel(other, base, src, out, buf, sem):
+    for _, store in every[-min(slots, count):]:
+        store.wait()
+
+
+def tail_kernel(lo, hi, other, base, src, out, sem):
     mi = lax.axis_index("mx")
     x, c = mi // 2, (mi + other) % 2
-    at = pl.multiple_of((2 * (1 - x) + c) * ROWS + NL * HALF, HALF)
-    rows = (NK - NL) * HALF // NN
-    moves = []
-    for i in range(NN):
-        to = out.at[pl.ds(at + i * rows, rows), pl.ds((NN - 1) * TN, TN)]
-        part = buf.at[pl.ds(i * rows, rows)]
-        moves.append((pltpu.make_async_copy(src.at[pl.ds(i * rows, rows)], part, sem.at[0, i]), pltpu.make_async_copy(part, to, sem.at[1, i])))
-    start_all(load for load, _ in moves)
-    for load, store in moves:
-        load.wait()
-        store.start()
-    wait_all(store for _, store in moves)
+    at = pl.multiple_of((2 * (1 - x) + c) * ROWS + lo * HALF, HALF)
+    move = pltpu.make_async_copy(src, out.at[pl.ds(at, (hi - lo) * HALF), pl.ds((NN - 1) * TN, TN)], sem)
+    move.start()
+    move.wait()
 
 
 def solution(mesh):
@@ -703,7 +727,7 @@
         tok = tokens.reshape(-1, WID)
         vecs = [v.reshape(-1, LANES) for v in (ln_scale, mlp_bias, q_scale, k_scale, attn_out_bias, mlp_out_bias)]
         of = lambda *shape: jax.ShapeDtypeStruct(shape, BF16)
-        shapes = [of(*tok.shape), of((NK - NL) * HALF, TN), of(ROWS, WID), of(3, WID, NJ * TN), of(4, WID, NJ * TN), of(3, JB, WID), of(4, JB, WID),
+        shapes = [of(*tok.shape), *[of((hi - lo) * HALF, TN) for lo, hi in TAILS], of(ROWS, WID), of(3, WID, NJ * TN), of(4, WID, NJ * TN), of(3, JB, WID), of(4, JB, WID),
                   of(3, NS, ROWS, TN), of(ROWS, NS * JB), of(ROWS, WID), of(ROWS, WID), of(ROWS, WID)]
         flops = 2 * ROWS * (2 * WID * NT * TN + NS * JB * 2 * WID)
         pairs = [(), (NK,), (7,), (7, NJ), (3,), (3, NN), (NS,), (NS, NN), (), (GROUPS, NN), (), (NK, NN), (2,), (2,), (NS,), (NS,)]
@@ -732,32 +756,50 @@
             cost_estimate=pl.CostEstimate(flops=flops, bytes_accessed=2**30, transcendentals=0),
             name="layer",
         )(tok, w_in, w_out, *vecs)
-        base, own = res[0], res[1]
-        far = lax.ppermute(own, 'mx', [(0, 2), (1, 3), (2, 0), (3, 1)])
-        base = pl.pallas_call(
-            copy_kernel,
-            out_shape=of(*tok.shape),
-            in_specs=[hbm],
-            out_specs=hbm,
-            scratch_shapes=[pltpu.VMEM((16, HALF, WID), BF16), dma(2, 16)],
-            compiler_params=pltpu.CompilerParams(vmem_limit_bytes=40 * 2**20),
-            cost_estimate=pl.CostEstimate(flops=2 * 10**10, bytes_accessed=4 * tok.size, transcendentals=0),
-            name="place",
-        )(base)
-        far, base = lax.optimization_barrier((far, base))
-        farther = lax.ppermute(far, 'mx', [(0, 1), (1, 0), (2, 3), (3, 2)])
-        for other, piece in enumerate((far, farther)):
-            base = pl.pallas_call(
-                functools.partial(tail_kernel, other),
+        base = res[0]
+        over_x = [(0, 2), (1, 3), (2, 0), (3, 1)]
+        over_core = [(0, 1), (1, 0), (2, 3), (3, 2)]
+        far = []
+        for own in res[1:3]:
+            far.append(lax.ppermute(own, 'mx', over_x))
+
+        def put(lo, hi, *arrays):
+            return pl.pallas_call(
+                functools.partial(copy_kernel, lo, hi),
                 out_shape=of(*tok.shape),
-                in_specs=[hbm] * 2,
+                in_specs=[hbm] * len(arrays),
+                out_specs=hbm,
+                input_output_aliases={i: 0 for i in range(1, len(arrays))},
+                scratch_shapes=[pltpu.VMEM((16, HALF, WID), BF16), dma(2, 16)],
+                compiler_params=pltpu.CompilerParams(vmem_limit_bytes=40 * 2**20),
+                cost_estimate=pl.CostEstimate(flops=(hi - lo) * 10**9, bytes_accessed=(hi - lo) * 4 * HALF * WID, transcendentals=0),
+                name="place",
+            )(*arrays)
+
+        def put_last(base, piece, lo, hi, other):
+            return pl.pallas_call(
+                functools.partial(tail_kernel, lo, hi, other),
+                out_shape=of(*tok.shape),
+                in_specs=[hbm, pl.BlockSpec(memory_space=pltpu.VMEM)],
                 out_specs=hbm,
                 input_output_aliases={0: 0},
-                scratch_shapes=[pltpu.VMEM(((NK - NL) * HALF, TN), BF16), dma(2, NN)],
+                scratch_shapes=[dma()],
+                compiler_params=pltpu.CompilerParams(vmem_limit_bytes=8 * 2**20),
                 cost_estimate=pl.CostEstimate(flops=10**9, bytes_accessed=4 * piece.size, transcendentals=0),
                 name="place_last",
             )(base, piece)
+
+        results = base
+        base = put(0, SPLIT, results)
+        for (lo, hi), piece in zip(TAILS, far):
+            piece, base = lax.optimization_barrier((piece, base))
+            farther = lax.ppermute(piece, 'mx', over_core)
+            if lo == NL:
+                base = put(SPLIT, 4 * NK, results, base)
+            for other, part in enumerate((piece, farther)):
+                base = put_last(base, part, lo, hi, other)
         return base.reshape(tokens.shape)
 
     specs_in = (P('dp', None, 'my'), P('my'), P('my', 'mx'), P('mx'), P(), P(), P('mx', 'my'), P('my'), P('my'))
+
     return jax.shard_map(local_layer, mesh=mesh, in_specs=specs_in, out_specs=P('dp', None, 'my'), check_vma=False)

time: 1460 us -> 1460 us (level)
    pallas_call x3 -> x6, Pallas kernels: 46.5 us -> 47.3 us  [the longest x2 43.3 us: put(): pl.pallas_call(functools.partial(copy_kernel, lo, hi), out_shape=of(*tok....]
  transfers between devices with their start and end apart: 2 -> 4, of which waited for: 2 -> 2; matrix products, arithmetic and copies ran while one was open for 0% -> 0% of each run, Pallas kernels for 3% -> 3%
where the time goes in v7:
time: 1460 us
  Pallas kernels  1450 us (99%)
    pallas_call x1, Pallas kernels, local_layer(): pl.pallas_call(kernel, out_shape=shapes, in_specs=[hbm] * 9, out_specs=[h...  1400 us
    pallas_call x2, Pallas kernels, put(): pl.pallas_call(functools.partial(copy_kernel, lo, hi), out_shape=of(*tok....  43.3 us
  transfers between devices with their start and end apart: 4, of which 2 were waited for; matrix products, arithmetic and copies ran while one was open for 0% of the time, Pallas kernels for 3%

profile of v7, /device:TPU:0, one launch (start us, length us, event | category | flops | bytes accessed | tf_op | source)
XLA Modules:
  0.0 1461.7 jit_solution(14534114373627780796)
XLA Ops:
  0.0 1405.0 %layer.1 = (bf16[16384,2048]{1,0:T(8,128)(2,1)}, bf16[1536,512]{1,0:T(8,128)(2,1)}, bf16[512,512]{1,0:T(8,128)(2,1)}, bf16[4096,2048]{1,0:T(8,128)(2,1)}, bf16[3...) custom-call(bf16[16384,2048]{1,0:T(8,128)(2,1)} %bitcast.tok, ...), custom_call_target="tpu_custom_call" | custom-call | flops 824633720832 | bytes 1073741824 | tf_op jit(solution)/shard_map/layer/pallas_call | solution.py:734
  1405.0 1.5 collective-permute-start.1
  1406.5 0.0 copy-start
  1406.5 37.9 %place.2.rest_0_ = bf16[16384,2048]{1,0:T(8,128)(2,1)} custom-call(bf16[16384,2048]{1,0:T(8,128)(2,1)} %get-tuple-element.13.src), custom_call_target="tpu_custom_call" | custom-call | flops 28000000000 | bytes 117440512 | tf_op jit(solution)/shard_map/place/pallas_call | solution.py:767
  1444.4 0.0 collective-permute-done.1.src
  1444.4 0.1 collective-permute-start.2
  1444.6 0.0 copy-done
  1444.6 0.5 collective-permute-start
  1445.1 5.4 place.3.base
  1450.5 1.2 place_last.4.base
  1451.7 0.0 collective-permute-done.2.src
  1451.7 1.2 place_last.5.base
  1452.8 6.0 collective-permute-done.src
  1458.8 0.0 collective-permute-start.3
  1458.8 0.8 place_last.6.base
  1459.6 1.1 collective-permute-done.3.src
  1460.7 0.8 place_last.7
Async XLA Ops:
  1405.0 39.5 %collective-permute-start.1 = (bf16[1536,512]{1,0:T(8,128)(2,1)}, bf16[1536,512]{1,0:T(8,128)(2,1)S(1)}, u32[]{:S(2)}, u32[]{:S(2)}) collective-permute-start(bf16[1536,512]{1,0:T(8,128)(2,1)} %get-tuple-element.14), channel_id=1, source_target_pairs={{0,2},{1,3},{2,0},{3,1},{4,6},{5,7},{6,4},{7,5}} | collective-permute-start | bytes 4718600 | tf_op jit(solution)/shard_map/ppermute | solution.py:764
  1406.5 38.1 %copy-start = (bf16[512,512]{1,0:T(8,128)(2,1)S(1)}, bf16[512,512]{1,0:T(8,128)(2,1)}, u32[]{:S(2)}) copy-start(bf16[512,512]{1,0:T(8,128)(2,1)} %get-tuple-element.12) | copy-start | bytes 1572868
  1444.4 7.2 collective-permute-start.2
  1444.6 14.2 collective-permute-start
  1458.8 1.9 collective-permute-start.3

commit v8 on v7

--- a/solution.py
+++ b/solution.py
@@ -44,7 +44,16 @@
     return pl.ds(pl.multiple_of(QKV + (UNITS // 2) * side, QKV), UNITS // 2)
 
 
+LAST = pl.ds((NN - 1) * TN, TN)
 PART_ROWS = (pl.ds(0, TN), pl.ds(TN, JB - TN))
+
+
+def first_row(x, c):
+    return pl.multiple_of((2 * x + c) * ROWS, ROWS)
+
+
+def cost(flops, size):
+    return pl.CostEstimate(flops=flops, bytes_accessed=size, transcendentals=0)
 
 
 def tile(n):
@@ -81,7 +90,7 @@
 
 
 def kernel(tok, w_in, w_out, lns, mb, qs, ks, ab, bb,
-           out, tail, tail2, toth, w1t, w1b, w2y, w2n, qkv, jb, pa, pb, ry,
+           out, tail, tail2, rec, toth, w1t, w1b, w2y, w2n, qkv, jb, pa, pb, ry,
            zj, wbuf, ptile, acc, abuf, sv, lbuf, sc, ub, gains, ob, raw, raw2,
            w1sem, w2sem, jsem, psem, asem, vsem, lsem, csem,
            t_s, t_r, w_s, w_r, e_s, e_r, d_s, d_r, y_s, y_r, x_s, x_r, o_s, o_r, m_s, m_r):
@@ -92,8 +101,7 @@
     dev_x = {"my": y, "mx": 2 * (1 - x) + c}
     dev_c = {"my": y, "mx": 2 * x + 1 - c}
     dev_d = {"my": y, "mx": 2 * (1 - x) + 1 - c}
-    row0 = (2 * x + c) * ROWS
-    row0_x = (2 * (1 - x) + c) * ROWS
+    row0, row0_x = first_row(x, c), first_row(1 - x, c)
 
     barrier = pltpu.get_barrier_semaphore()
     for dev in (dev_y, dev_x, dev_c, dev_d):
@@ -522,6 +530,13 @@
         def _():
             to(tail2).start()
 
+    def is_last(k, n):
+        return (n == NN - 1) & (k == NL - 1)
+
+    def o_rec():
+        at = out.at[own_out(NL - 1), LAST]
+        return remote(at, rec, x_s, x_r.at[NL - 1, NN - 1], dev_x)
+
     def is_tail(k, n):
         return (n == NN - 1) & (k >= NL)
 
@@ -549,7 +564,11 @@
         def _():
             pltpu.make_async_copy(sv.at[e, 3], tail2, vsem.at[e, 4]).wait()
 
-        @pl.when(jnp.logical_not(is_tail(k, n)))
+        @pl.when(is_last(k, n))
+        def _():
+            o_rec().start()
+
+        @pl.when(jnp.logical_not(is_tail(k, n) | is_last(k, n)))
         def _():
             o_x(k, n).start()
 
@@ -667,35 +686,46 @@
     for kind in range(NS - 1):
         remote(theirs[OWN], theirs[OWN], e_s.at[kind], e_s.at[kind], dev_y).wait_send()
     remote(pb, pb, y_s, y_s, dev_y).wait_send()
-    mine_out = out.at[pl.ds(pl.multiple_of(row0, ROWS), ROWS)]
+    mine_out = out.at[pl.ds(row0, ROWS)]
     near_out = remote(mine_out, mine_out, o_s.at[0], o_r.at[0], dev_c)
     near_out.wait_send()
     near_out.wait_recv()
 
-    loop(0, NK - NL, lambda k: hand_out(k, NN - 1))
-    sent = out.at[pl.ds(pl.multiple_of(row0, ROWS), ROWS - (NK - NL) * HALF // NN)]
-    remote(sent, sent, x_s, x_s, dev_x).wait_send()
-    far_out = remote(sent, sent, o_s.at[1], o_r.at[1], dev_c)
+    loop(0, NL - 1, lambda k: hand_out(k, NN - 1))
+    crossed = ROWS - (NK - NL) * HALF // NN
+    handed = out.at[pl.ds(row0, crossed - HALF // NN)]
+    sent = out.at[pl.ds(row0, crossed)]
+    far_out = remote(handed, handed, o_s.at[1], o_r.at[1], dev_c)
     far_out.wait_send()
     far_out.wait_recv()
+    o_rec().wait_recv()
+    remote(sent, sent, x_s, x_s, dev_x).wait_send()
 
 
 def copy_kernel(lo, hi, src, *rest):
-    dst, buf, sem = rest[-3:]
+    more, (dst, buf, sem) = rest[1:-3], rest[-3:]
     slots = buf.shape[0]
     x = lax.axis_index("mx") // 2
 
     def moves(i):
         first = (x + i // (2 * NK)) % 2
-        rows = pl.ds(pl.multiple_of(first * 2 * ROWS + (i % (2 * NK)) * HALF, HALF), HALF)
+        rows = pl.ds(pl.multiple_of(first_row(first, (i // NK) % 2) + (i % NK) * HALF, HALF), HALF)
         late = i >= 2 * NK and i % NK >= NL
         cols = pl.ds(0, WID - TN if late else WID)
         k = (i - lo) % slots
         return (pltpu.make_async_copy(src.at[rows, cols], buf.at[k, :, cols], sem.at[0, k]),
                 pltpu.make_async_copy(buf.at[k, :, cols], dst.at[rows, cols], sem.at[1, k]))
 
-    every = [moves(i) for i in range(lo, hi)]
-    ahead, count = 12, hi - lo
+    def one_more(i, ref):
+        c = (lax.axis_index("mx") + i) % 2
+        rows = pl.ds(pl.multiple_of(first_row(1 - x, c) + (NL - 1) * HALF, HALF), HALF)
+        cols = LAST
+        k = (hi - lo + i) % slots
+        return (pltpu.make_async_copy(ref, buf.at[k, :, cols], sem.at[0, k]),
+                pltpu.make_async_copy(buf.at[k, :, cols], dst.at[rows, cols], sem.at[1, k]))
+
+    every = [moves(i) for i in range(lo, hi)] + [one_more(i, ref) for i, ref in enumerate(more)]
+    ahead, count = 12, len(every)
     for i in range(count + ahead):
         if i < count:
             if i >= slots:
@@ -708,13 +738,15 @@
         store.wait()
 
 
-def tail_kernel(lo, hi, other, base, src, out, sem):
+def tail_kernel(lo, hi, others, base, *rest):
+    pieces, (out, sem) = rest[:-2], rest[-2:]
     mi = lax.axis_index("mx")
-    x, c = mi // 2, (mi + other) % 2
-    at = pl.multiple_of((2 * (1 - x) + c) * ROWS + lo * HALF, HALF)
-    move = pltpu.make_async_copy(src, out.at[pl.ds(at, (hi - lo) * HALF), pl.ds((NN - 1) * TN, TN)], sem)
-    move.start()
-    move.wait()
+    moves = []
+    for i, (other, piece) in enumerate(zip(others, pieces)):
+        at = pl.multiple_of(first_row(1 - mi // 2, (mi + other) % 2) + lo * HALF, HALF)
+        moves.append(pltpu.make_async_copy(piece, out.at[pl.ds(at, (hi - lo) * HALF), LAST], sem.at[i]))
+    start_all(moves)
+    wait_all(moves)
 
 
 def solution(mesh):
@@ -727,7 +759,7 @@
         tok = tokens.reshape(-1, WID)
         vecs = [v.reshape(-1, LANES) for v in (ln_scale, mlp_bias, q_scale, k_scale, attn_out_bias, mlp_out_bias)]
         of = lambda *shape: jax.ShapeDtypeStruct(shape, BF16)
-        shapes = [of(*tok.shape), *[of((hi - lo) * HALF, TN) for lo, hi in TAILS], of(ROWS, WID), of(3, WID, NJ * TN), of(4, WID, NJ * TN), of(3, JB, WID), of(4, JB, WID),
+        shapes = [of(*tok.shape), *[of((hi - lo) * HALF, TN) for lo, hi in TAILS], of(HALF, TN), of(ROWS, WID), of(3, WID, NJ * TN), of(4, WID, NJ * TN), of(3, JB, WID), of(4, JB, WID),
                   of(3, NS, ROWS, TN), of(ROWS, NS * JB), of(ROWS, WID), of(ROWS, WID), of(ROWS, WID)]
         flops = 2 * ROWS * (2 * WID * NT * TN + NS * JB * 2 * WID)
         pairs = [(), (NK,), (7,), (7, NJ), (3,), (3, NN), (NS,), (NS, NN), (), (GROUPS, NN), (), (NK, NN), (2,), (2,), (NS,), (NS,)]
@@ -753,12 +785,12 @@
                 dma(2, 2), dma(2, 5), dma(2), dma(2), dma(2, 3), dma(2, 5), dma(2, 2), dma(6),
             ] + [dma(*shape) for shape in pairs],
             compiler_params=pltpu.CompilerParams(collective_id=0, has_side_effects=True, vmem_limit_bytes=63 * 2**20),
-            cost_estimate=pl.CostEstimate(flops=flops, bytes_accessed=2**30, transcendentals=0),
+            cost_estimate=cost(flops, 2**30),
             name="layer",
         )(tok, w_in, w_out, *vecs)
         base = res[0]
-        over_x = [(0, 2), (1, 3), (2, 0), (3, 1)]
-        over_core = [(0, 1), (1, 0), (2, 3), (3, 2)]
+        over_x = [(i, i ^ 2) for i in range(NS)]
+        over_core = [(i, i ^ 1) for i in range(NS)]
         far = []
         for own in res[1:3]:
             far.append(lax.ppermute(own, 'mx', over_x))
@@ -769,35 +801,38 @@
                 out_shape=of(*tok.shape),
                 in_specs=[hbm] * len(arrays),
                 out_specs=hbm,
-                input_output_aliases={i: 0 for i in range(1, len(arrays))},
+                input_output_aliases={i: 0 for i in range(1, min(2, len(arrays)))},
                 scratch_shapes=[pltpu.VMEM((16, HALF, WID), BF16), dma(2, 16)],
                 compiler_params=pltpu.CompilerParams(vmem_limit_bytes=40 * 2**20),
-                cost_estimate=pl.CostEstimate(flops=(hi - lo) * 10**9, bytes_accessed=(hi - lo) * 4 * HALF * WID, transcendentals=0),
+                cost_estimate=cost((hi - lo) * 10**9, (hi - lo) * 4 * HALF * WID),
                 name="place",
             )(*arrays)
 
-        def put_last(base, piece, lo, hi, other):
+        def put_last(base, lo, hi, others, *pieces):
             return pl.pallas_call(
-                functools.partial(tail_kernel, lo, hi, other),
+                functools.partial(tail_kernel, lo, hi, others),
                 out_shape=of(*tok.shape),
-                in_specs=[hbm, pl.BlockSpec(memory_space=pltpu.VMEM)],
+                in_specs=[hbm] + [pl.BlockSpec(memory_space=pltpu.VMEM)] * len(pieces),
                 out_specs=hbm,
                 input_output_aliases={0: 0},
-                scratch_shapes=[dma()],
+                scratch_shapes=[dma(2)],
                 compiler_params=pltpu.CompilerParams(vmem_limit_bytes=8 * 2**20),
-                cost_estimate=pl.CostEstimate(flops=10**9, bytes_accessed=4 * piece.size, transcendentals=0),
+                cost_estimate=cost(10**9, 8 * pieces[0].size),
                 name="place_last",
-            )(base, piece)
-
-        results = base
+            )(base, *pieces)
+
+        results, rec = base, res[3]
+        rec_near = lax.ppermute(rec, 'mx', over_core)
         base = put(0, SPLIT, results)
         for (lo, hi), piece in zip(TAILS, far):
             piece, base = lax.optimization_barrier((piece, base))
             farther = lax.ppermute(piece, 'mx', over_core)
             if lo == NL:
-                base = put(SPLIT, 4 * NK, results, base)
-            for other, part in enumerate((piece, farther)):
-                base = put_last(base, part, lo, hi, other)
+                base = put(SPLIT, 4 * NK, results, base, rec, rec_near)
+                base = put_last(base, lo, hi, (0, 1), piece, farther)
+            else:
+                base = put_last(base, lo, hi, (0,), piece)
+                base = put_last(base, lo, hi, (1,), farther)
         return base.reshape(tokens.shape)
 
     specs_in = (P('dp', None, 'my'), P('my'), P('my', 'mx'), P('mx'), P(), P(), P('mx', 'my'), P('my'), P('my'))

time: 1460 us -> 1460 us (level)
  transfers between devices with their start and end apart: 4 -> 5, of which waited for: 2 -> 3; matrix products, arithmetic and copies ran while one was open for 0% -> 0% of each run, Pallas kernels for 3% -> 3%
where the time goes in v8:
time: 1460 us
  Pallas kernels  1450 us (99%)
    pallas_call x1, Pallas kernels, local_layer(): pl.pallas_call(kernel, out_shape=shapes, in_specs=[hbm] * 9, out_specs=[h...  1400 us
    pallas_call x2, Pallas kernels, put(): pl.pallas_call(functools.partial(copy_kernel, lo, hi), out_shape=of(*tok....  43.7 us
  transfers between devices with their start and end apart: 5, of which 3 were waited for; matrix products, arithmetic and copies ran while one was open for 0% of the time, Pallas kernels for 3%

profile of v8, /device:TPU:0, one launch (start us, length us, event | category | flops | bytes accessed | tf_op | source)
XLA Modules:
  0.0 1459.9 jit_solution(10484304560819056018)
XLA Ops:
  0.0 1403.1 %layer.1 = (bf16[16384,2048]{1,0:T(8,128)(2,1)}, bf16[1536,512]{1,0:T(8,128)(2,1)}, bf16[512,512]{1,0:T(8,128)(2,1)}, bf16[512,512]{1,0:T(8,128)(2,1)}, bf16[409...) custom-call(bf16[16384,2048]{1,0:T(8,128)(2,1)} %bitcast.tok, ...), custom_call_target="tpu_custom_call" | custom-call | flops 824633720832 | bytes 1073741824 | tf_op jit(solution)/shard_map/layer/pallas_call | solution.py:766
  1403.1 1.5 collective-permute-start.1
  1404.6 0.0 copy-start
  1404.6 0.0 copy-start.1
  1404.6 38.0 %place.2.rest_0_ = bf16[16384,2048]{1,0:T(8,128)(2,1)} custom-call(bf16[16384,2048]{1,0:T(8,128)(2,1)} %get-tuple-element.14.src), custom_call_target="tpu_custom_call" | custom-call | flops 28000000000 | bytes 117440512 | tf_op jit(solution)/shard_map/place/pallas_call | solution.py:799
  1442.6 0.0 collective-permute-done.1.rest_0_
  1442.6 0.0 collective-permute-start.3
  1442.6 0.0 copy-done
  1442.6 0.5 collective-permute-start.2
  1443.1 0.0 copy-done.1
  1443.1 0.5 collective-permute-start
  1443.7 3.1 collective-permute-done.2.rest_2_
  1446.8 5.7 place.3.base
  1452.5 0.0 collective-permute-done.3.rest_1_
  1452.5 1.7 place_last.3.base
  1454.2 2.8 collective-permute-done.rest_0_
  1457.0 0.0 collective-permute-start.4
  1457.0 0.8 place_last.4.base
  1457.8 1.1 collective-permute-done.4.rest_0_
  1458.9 0.8 place_last.5
Async XLA Ops:
  1403.1 39.5 %collective-permute-start.1 = (bf16[1536,512]{1,0:T(8,128)(2,1)}, bf16[1536,512]{1,0:T(8,128)(2,1)S(1)}, u32[]{:S(2)}, u32[]{:S(2)}) collective-permute-start(bf16[1536,512]{1,0:T(8,128)(2,1)} %get-tuple-element.15), channel_id=1, source_target_pairs={{0,2},{1,3},{2,0},{3,1},{4,6},{5,7},{6,4},{7,5}} | collective-permute-start | bytes 4718600 | tf_op jit(solution)/shard_map/ppermute | solution.py:796
  1404.6 38.0 %copy-start = (bf16[512,512]{1,0:T(8,128)(2,1)S(1)}, bf16[512,512]{1,0:T(8,128)(2,1)}, u32[]{:S(2)}) copy-start(bf16[512,512]{1,0:T(8,128)(2,1)} %get-tuple-element.17.rest_1_) | copy-start | bytes 1572868
  1404.6 38.5 %copy-start.1 = (bf16[512,512]{1,0:T(8,128)(2,1)S(1)}, bf16[512,512]{1,0:T(8,128)(2,1)}, u32[]{:S(2)}) copy-start(bf16[512,512]{1,0:T(8,128)(2,1)} %get-tuple-element.13) | copy-start | bytes 1572868
  1442.6 9.9 collective-permute-start.3
  1442.6 4.1 collective-permute-start.2
  1443.1 13.9 collective-permute-start
  1457.0 1.9 collective-permute-start.4

commit v9 on v8

--- a/solution.py
+++ b/solution.py
@@ -29,7 +29,7 @@
 NK = 2 * GROUPS
 NL = NK // 2
 TAILS = ((NL, NK - 1), (NK - 1, NK))
-SPLIT = 3 * NK + NL
+SPLIT = 4 * NK - 2
 
 
 def in_col(j, side):
@@ -824,15 +824,13 @@
         results, rec = base, res[3]
         rec_near = lax.ppermute(rec, 'mx', over_core)
         base = put(0, SPLIT, results)
-        for (lo, hi), piece in zip(TAILS, far):
-            piece, base = lax.optimization_barrier((piece, base))
-            farther = lax.ppermute(piece, 'mx', over_core)
-            if lo == NL:
-                base = put(SPLIT, 4 * NK, results, base, rec, rec_near)
-                base = put_last(base, lo, hi, (0, 1), piece, farther)
-            else:
-                base = put_last(base, lo, hi, (0,), piece)
-                base = put_last(base, lo, hi, (1,), farther)
+        first, base = lax.optimization_barrier((far[0], base))
+        first_near = lax.ppermute(first, 'mx', over_core)
+        base = put(SPLIT, 4 * NK, results, base, rec, rec_near)
+        second, first_near, base = lax.optimization_barrier((far[1], first_near, base))
+        second_near = lax.ppermute(second, 'mx', over_core)
+        for (lo, hi), pieces in zip(TAILS, ((first, first_near), (second, second_near))):
+            base = put_last(base, lo, hi, range(2), *pieces)
         return base.reshape(tokens.shape)
 
     specs_in = (P('dp', None, 'my'), P('my'), P('my', 'mx'), P('mx'), P(), P(), P('mx', 'my'), P('my'), P('my'))

time: 1460 us -> 1460 us (level)
  no operation moved by 1% of the time
where the time goes in v9:
time: 1460 us
  Pallas kernels  1450 us (99%)
    pallas_call x1, Pallas kernels, local_layer(): pl.pallas_call(kernel, out_shape=shapes, in_specs=[hbm] * 9, out_specs=[h...  1400 us
    pallas_call x2, Pallas kernels, put(): pl.pallas_call(functools.partial(copy_kernel, lo, hi), out_shape=of(*tok....  43.2 us
  transfers between devices with their start and end apart: 5, of which 3 were waited for; matrix products, arithmetic and copies ran while one was open for 0% of the time, Pallas kernels for 3%

profile of v9, /device:TPU:0, one launch (start us, length us, event | category | flops | bytes accessed | tf_op | source)
XLA Modules:
  0.0 1461.6 jit_solution(8832028627990825327)
XLA Ops:
  0.0 1403.1 %layer.1 = (bf16[16384,2048]{1,0:T(8,128)(2,1)}, bf16[1536,512]{1,0:T(8,128)(2,1)}, bf16[512,512]{1,0:T(8,128)(2,1)}, bf16[512,512]{1,0:T(8,128)(2,1)}, bf16[409...) custom-call(bf16[16384,2048]{1,0:T(8,128)(2,1)} %bitcast.tok, ...), custom_call_target="tpu_custom_call" | custom-call | flops 824633720832 | bytes 1073741824 | tf_op jit(solution)/shard_map/layer/pallas_call | solution.py:766
  1403.1 1.5 collective-permute-start.1
  1404.6 0.0 copy-start
  1404.6 0.0 copy-start.1
  1404.6 39.5 %place.2.rest_0_ = bf16[16384,2048]{1,0:T(8,128)(2,1)} custom-call(bf16[16384,2048]{1,0:T(8,128)(2,1)} %get-tuple-element.16.src), custom_call_target="tpu_custom_call" | custom-call | flops 30000001024 | bytes 125829120 | tf_op jit(solution)/shard_map/place/pallas_call | solution.py:799
  1444.1 0.0 collective-permute-done.1.rest_0_
  1444.1 0.0 collective-permute-start.2
  1444.2 0.0 copy-done
  1444.2 0.5 collective-permute-start.3
  1444.7 0.0 copy-done.1
  1444.7 0.5 collective-permute-start
  1445.2 3.1 collective-permute-done.3.rest_2_
  1448.3 3.7 place.3.base
  1452.0 6.5 collective-permute-done.rest_0_
  1458.5 0.0 collective-permute-done.2.rest_1_
  1458.5 0.0 collective-permute-start.4
  1458.6 1.7 place_last.2.base
  1460.2 0.2 collective-permute-done.4.rest_1_
  1460.5 1.0 place_last.3
Async XLA Ops:
  1403.1 41.0 %collective-permute-start.1 = (bf16[1536,512]{1,0:T(8,128)(2,1)}, bf16[1536,512]{1,0:T(8,128)(2,1)S(1)}, u32[]{:S(2)}, u32[]{:S(2)}) collective-permute-start(bf16[1536,512]{1,0:T(8,128)(2,1)} %get-tuple-element.15), channel_id=1, source_target_pairs={{0,2},{1,3},{2,0},{3,1},{4,6},{5,7},{6,4},{7,5}} | collective-permute-start | bytes 4718600 | tf_op jit(solution)/shard_map/ppermute | solution.py:796
  1404.6 39.6 %copy-start = (bf16[512,512]{1,0:T(8,128)(2,1)S(1)}, bf16[512,512]{1,0:T(8,128)(2,1)}, u32[]{:S(2)}) copy-start(bf16[512,512]{1,0:T(8,128)(2,1)} %get-tuple-element.19.rest_1_) | copy-start | bytes 1572868
  1404.6 40.1 %copy-start.1 = (bf16[512,512]{1,0:T(8,128)(2,1)S(1)}, bf16[512,512]{1,0:T(8,128)(2,1)}, u32[]{:S(2)}) copy-start(bf16[512,512]{1,0:T(8,128)(2,1)} %get-tuple-element.14) | copy-start | bytes 1572868
  1444.1 14.4 collective-permute-start.2
  1444.2 4.1 collective-permute-start.3
  1444.7 13.9 collective-permute-start
  1458.5 1.9 collective-permute-start.4

commit v10 on v9

--- a/solution.py
+++ b/solution.py
@@ -725,7 +725,7 @@
                 pltpu.make_async_copy(buf.at[k, :, cols], dst.at[rows, cols], sem.at[1, k]))
 
     every = [moves(i) for i in range(lo, hi)] + [one_more(i, ref) for i, ref in enumerate(more)]
-    ahead, count = 12, len(every)
+    ahead, count = 6, len(every)
     for i in range(count + ahead):
         if i < count:
             if i >= slots:
@@ -802,8 +802,8 @@
                 in_specs=[hbm] * len(arrays),
                 out_specs=hbm,
                 input_output_aliases={i: 0 for i in range(1, min(2, len(arrays)))},
-                scratch_shapes=[pltpu.VMEM((16, HALF, WID), BF16), dma(2, 16)],
-                compiler_params=pltpu.CompilerParams(vmem_limit_bytes=40 * 2**20),
+                scratch_shapes=[pltpu.VMEM((8, HALF, WID), BF16), dma(2, 8)],
+                compiler_params=pltpu.CompilerParams(vmem_limit_bytes=20 * 2**20),
                 cost_estimate=cost((hi - lo) * 10**9, (hi - lo) * 4 * HALF * WID),
                 name="place",
             )(*arrays)

time: 1460 us -> 1460 us (level)
  no operation moved by 1% of the time
where the time goes in v10:
time: 1460 us
  Pallas kernels  1450 us (99%)
    pallas_call x1, Pallas kernels, local_layer(): pl.pallas_call(kernel, out_shape=shapes, in_specs=[hbm] * 9, out_specs=[h...  1400 us
    pallas_call x2, Pallas kernels, put(): pl.pallas_call(functools.partial(copy_kernel, lo, hi), out_shape=of(*tok....  43 us
  transfers between devices with their start and end apart: 5, of which 3 were waited for; matrix products, arithmetic and copies ran while one was open for 0% of the time, Pallas kernels for 3%

profile of v10, /device:TPU:0, one launch (start us, length us, event | category | flops | bytes accessed | tf_op | source)
XLA Modules:
  0.0 1461.6 jit_solution(17924731948712255950)
XLA Ops:
  0.0 1403.1 %layer.1 = (bf16[16384,2048]{1,0:T(8,128)(2,1)}, bf16[1536,512]{1,0:T(8,128)(2,1)}, bf16[512,512]{1,0:T(8,128)(2,1)}, bf16[512,512]{1,0:T(8,128)(2,1)}, bf16[409...) custom-call(bf16[16384,2048]{1,0:T(8,128)(2,1)} %bitcast.tok, ...), custom_call_target="tpu_custom_call" | custom-call | flops 824633720832 | bytes 1073741824 | tf_op jit(solution)/shard_map/layer/pallas_call | solution.py:766
  1403.1 1.5 collective-permute-start.1
  1404.6 0.0 copy-start
  1404.6 0.0 copy-start.1
  1404.6 39.5 %place.2.rest_0_ = bf16[16384,2048]{1,0:T(8,128)(2,1)} custom-call(bf16[16384,2048]{1,0:T(8,128)(2,1)} %get-tuple-element.16.src), custom_call_target="tpu_custom_call" | custom-call | flops 30000001024 | bytes 125829120 | tf_op jit(solution)/shard_map/place/pallas_call | solution.py:799
  1444.1 0.0 collective-permute-done.1.rest_0_
  1444.1 0.0 collective-permute-start.2
  1444.1 0.0 copy-done
  1444.1 0.5 collective-permute-start.3
  1444.6 0.0 copy-done.1
  1444.6 0.5 collective-permute-start
  1445.2 3.1 collective-permute-done.3.rest_2_
  1448.3 3.5 place.3.base
  1451.8 6.7 collective-permute-done.rest_0_
  1458.5 0.0 collective-permute-done.2.rest_1_
  1458.5 0.0 collective-permute-start.4
  1458.5 1.7 place_last.2.base
  1460.2 0.2 collective-permute-done.4.rest_1_
  1460.4 1.0 place_last.3
Async XLA Ops:
  1403.1 41.0 %collective-permute-start.1 = (bf16[1536,512]{1,0:T(8,128)(2,1)}, bf16[1536,512]{1,0:T(8,128)(2,1)S(1)}, u32[]{:S(2)}, u32[]{:S(2)}) collective-permute-start(bf16[1536,512]{1,0:T(8,128)(2,1)} %get-tuple-element.15), channel_id=1, source_target_pairs={{0,2},{1,3},{2,0},{3,1},{4,6},{5,7},{6,4},{7,5}} | collective-permute-start | bytes 4718600 | tf_op jit(solution)/shard_map/ppermute | solution.py:796
  1404.6 39.5 %copy-start = (bf16[512,512]{1,0:T(8,128)(2,1)S(1)}, bf16[512,512]{1,0:T(8,128)(2,1)}, u32[]{:S(2)}) copy-start(bf16[512,512]{1,0:T(8,128)(2,1)} %get-tuple-element.19.rest_1_) | copy-start | bytes 1572868
  1404.6 40.0 %copy-start.1 = (bf16[512,512]{1,0:T(8,128)(2,1)S(1)}, bf16[512,512]{1,0:T(8,128)(2,1)}, u32[]{:S(2)}) copy-start(bf16[512,512]{1,0:T(8,128)(2,1)} %get-tuple-element.14) | copy-start | bytes 1572868
  1444.1 14.4 collective-permute-start.2
  1444.1 4.1 collective-permute-start.3
  1444.6 13.9 collective-permute-start
  1458.5 1.9 collective-permute-start.4
